TPU v7x, 128 devices: a whole 4x4x4 slice. The times are simulated.
128 devices in a mesh: dp: 16 (over y_hi, z, core), tensor: 8 (over y_lo, x).
Axes of the slice: x: 4, y: 4 (y_hi: 2, y_lo: 2; y = y_hi * 2 + y_lo), z: 4, core: 2. Of those that a mesh axis runs over, the one named last changes fastest.
Arguments:
- saved_queries: bfloat16 [16384, 8192], P('dp', 'tensor'), may hold values from -200 to 200
- saved_keys: bfloat16 [16384, 1024], P('dp', 'tensor'), may hold values from -200 to 200
- saved_values: bfloat16 [16384, 1024], P('dp', 'tensor'), may hold values from -6 to 6
- out_grad: bfloat16 [16384, 8192], P(('dp', 'tensor')), may hold values from -2.5 to 2.5
- act_exponent: int32 [1], replicated, may hold values from -6 to 3
- grad_exponent: int32 [1], replicated, may hold values from -4 to 1
Outputs:
- grad_weight: float32 [8192, 8192], P('dp', 'tensor')
All inputs are finite; a program needn't handle non-finite values.
Results may differ from a plain program's by a relative error of at most 0.012.
Values may be sent and summed in bfloat16 or wider, within the bound.
No kernel may reach another device: no remote copies, remote signals or barrier semaphores. Data moves between devices by JAX's collectives and lax.ppermute only.
A program may use at most 128 MiB of HBM per device.

v0:
```python
import functools

import jax
import jax.numpy as jnp
from jax import lax
from jax.experimental import pallas as pl
from jax.experimental.pallas import tpu as pltpu
from jax.sharding import PartitionSpec as P


HEAD_DIM = 128
SATURATION = 448.0
NY, NZ, NC, NX = 2, 4, 2, 4
AXES = ("dp", "tensor")
UNITS = 4
ROWS = 128
STEPS = (2, 1, 3, 0)
QUARTER = 256


def device_of(yh, z, c, yl, x):
    return ((yh * NZ + z) * NC + c) * (NY * NX) + yl * NX + x


def pairs_of(target):
    pairs = []
    for yh in range(NY):
        for z in range(NZ):
            for c in range(NC):
                for yl in range(NY):
                    for x in range(NX):
                        pairs.append((device_of(yh, z, c, yl, x), device_of(*target(yh, z, c, yl, x))))
    return pairs


X_UP = pairs_of(lambda yh, z, c, yl, x: (yh, z, c, yl, (x + 1) % NX))
X_DOWN = pairs_of(lambda yh, z, c, yl, x: (yh, z, c, yl, (x - 1) % NX))
Z_UP = pairs_of(lambda yh, z, c, yl, x: (yh, (z + 1) % NZ, c, yl, x))
Z_DOWN = pairs_of(lambda yh, z, c, yl, x: (yh, (z - 1) % NZ, c, yl, x))
Y_INNER = pairs_of(lambda yh, z, c, yl, x: (yh, z, c, 1 - yl, x))
Y_OUTER = pairs_of(lambda yh, z, c, yl, x: (1 - yh, z, c, 1 - yl, x))
CORES = pairs_of(lambda yh, z, c, yl, x: (yh, z, 1 - c, yl, x))


def send(block, pairs):
    return lax.ppermute(block, AXES, pairs)


def position():
    place = lax.axis_index("dp")
    side = lax.axis_index("tensor")
    return place // (NZ * NC), place // NC % NZ, place % NC, side // NX, side % NX


def saturation_factor(exponent_ref, width):
    exponent = jnp.full((1, width), -exponent_ref[0].astype(jnp.float32))
    return SATURATION * jnp.exp2(exponent)


GROUPS = ((0, 1), (1, 1), (2, 2))
FIRST = ((1, 1, 0, 1), (0, 1, 0, 1), (1, 0, 0, 1), (0, 0, 0, 1))
REST = ((1, 0, 1, 3), (1, 1, 1, 1), (1, 1, 2, 2)) + tuple((0, 0, u, 1) for u in (1, 2, 3)) + ((0, 1, 1, 1), (0, 1, 2, 2))


def quantize_kernel(exponent_ref, grad_ref, *out_refs, made):
    yh, z, c, yl, _ = position()
    factor = saturation_factor(exponent_ref, ROWS)
    for (other_core, far_chip, first, count), ref in zip(made, out_refs, strict=True):
        chip = (yl ^ yh) ^ far_chip
        core = c ^ other_core
        for unit in range(first, first + count):
            for step in range(NZ):
                yh_at = yh if unit % 2 else 1 - yh
                z_at = lax.rem(z + STEPS[step], NZ)
                column = 4 * (8 * yh_at + 2 * z_at + chip) + 2 * core + unit // 2
                values = grad_ref[:, pl.ds(pl.multiple_of(column * ROWS, ROWS), ROWS)].astype(jnp.float32)
                scaled = jnp.clip(values * factor, -SATURATION, SATURATION).astype(jnp.bfloat16)
                ref[unit - first, step * ROWS : (step + 1) * ROWS, :] = scaled.T


def quantize_columns(exponent, out_grad, made):
    tokens = out_grad.shape[0]
    arrays = pl.pallas_call(
        functools.partial(quantize_kernel, made=made),
        in_specs=[pl.BlockSpec(memory_space=pltpu.SMEM), pl.BlockSpec(memory_space=pltpu.VMEM)],
        out_specs=[pl.BlockSpec(memory_space=pltpu.VMEM)] * len(made),
        out_shape=[jax.ShapeDtypeStruct((n, NZ * ROWS, tokens), jnp.bfloat16) for *_, n in made],
        cost_estimate=pl.CostEstimate(flops=2 * 10**9, bytes_accessed=3 * 2**20, transcendentals=0),
    )(exponent, out_grad)
    return dict(zip(made, arrays, strict=True))


Q_BLOCK = 256


def attention_kernel(exponent_ref, query_ref, key_ref, value_ref, out_ref):
    _, _, _, _, x = position()
    seq_len = key_ref.shape[0]
    scale = HEAD_DIM**-0.5
    factor = saturation_factor(exponent_ref, HEAD_DIM)
    row = lax.broadcasted_iota(jnp.int32, (Q_BLOCK, Q_BLOCK), 0)
    column = lax.broadcasted_iota(jnp.int32, (Q_BLOCK, Q_BLOCK), 1)
    causal = column <= row
    for start in range(0, seq_len, Q_BLOCK):
        queries = query_ref[start : start + Q_BLOCK, :]

        def scores_of(first, last):
            return lax.dot_general(
                queries, key_ref[first:last, :], (((1,), (1,)), ((), ())), preferred_element_type=jnp.float32
            )

        near = jnp.where(causal, scores_of(start, start + Q_BLOCK), jnp.float32(-1e30))
        row_max = jnp.max(near, axis=1, keepdims=True)
        if start:
            past = scores_of(0, start)
            row_max = jnp.maximum(row_max, jnp.max(past, axis=1, keepdims=True))
        weights = jnp.exp((near - row_max) * scale)
        total = jnp.sum(weights, axis=1, keepdims=True)
        mixed = jnp.dot(
            weights.astype(jnp.bfloat16), value_ref[start : start + Q_BLOCK, :], preferred_element_type=jnp.float32
        )
        if start:
            weights = jnp.exp((past - row_max) * scale)
            total = total + jnp.sum(weights, axis=1, keepdims=True)
            mixed = mixed + jnp.dot(
                weights.astype(jnp.bfloat16), value_ref[:start, :], preferred_element_type=jnp.float32
            )
        scaled = jnp.clip(mixed / total * factor, -SATURATION, SATURATION).astype(jnp.bfloat16)
        for part in range(Q_BLOCK // ROWS):
            token_block = start // ROWS + part
            ahead = lax.rem(token_block % NX - x + NX, NX)
            order = jnp.where(ahead == 0, 0, jnp.where(ahead == 3, 1, ahead + 1))
            out_ref[pl.ds(order * 2 + token_block // NX, 1)] = scaled[part * ROWS : (part + 1) * ROWS][None]


def attend(exponent, queries, keys, values, first, heads):
    seq_len = queries.shape[0]
    blocks = seq_len // ROWS
    return pl.pallas_call(
        attention_kernel,
        grid=(heads,),
        in_specs=[
            pl.BlockSpec(memory_space=pltpu.SMEM),
            pl.BlockSpec((seq_len, HEAD_DIM), lambda h: (0, h + first)),
            pl.BlockSpec((seq_len, HEAD_DIM), lambda h: (0, 0)),
            pl.BlockSpec((seq_len, HEAD_DIM), lambda h: (0, 0)),
        ],
        out_specs=pl.BlockSpec((blocks, ROWS, HEAD_DIM), lambda h: (0, 0, h)),
        out_shape=jax.ShapeDtypeStruct((blocks, ROWS, heads * HEAD_DIM), jnp.bfloat16),
        cost_estimate=pl.CostEstimate(flops=4 * 10**9, bytes_accessed=2**20, transcendentals=0),
    )(exponent, queries, keys, values)


def product_kernel(*refs, jobs, units, acts):
    piece_refs = [refs[4 * u : 4 * u + 4] for u in range(units)]
    act_refs = [refs[4 * units + 2 * a : 4 * units + 2 * a + 2] for a in range(acts // 2)]
    outs = refs[4 * units + acts : 4 * units + acts + 4]
    grads, values, results, grad_sem, value_sem, result_sem = refs[4 * units + acts + 4 :]
    yl = position()[3]
    grad_copies = []
    for u in range(units):
        for seq in range(2):
            for source in range(NX):
                for row in range(2):
                    at = (seq * NX + source) * 2 + row
                    grad_copies.append(
                        pltpu.make_async_copy(
                            piece_refs[u][source].at[seq, row ^ yl],
                            grads.at[u, :, pl.ds(at * ROWS, ROWS)],
                            grad_sem.at[u, at],
                        )
                    )
    value_copies = [
        pltpu.make_async_copy(
            act_refs[a // 2][seq].at[:, :, pl.ds(a % 2 * QUARTER, QUARTER)], values.at[a, seq], value_sem.at[a, seq]
        )
        for a in range(acts)
        for seq in range(2)
    ]
    per_unit = len(grad_copies) // units
    for copy in grad_copies[:per_unit] + value_copies + grad_copies[per_unit:]:
        copy.start()
    waited = 0
    done = 0
    for u in range(units):
        for copy in grad_copies[u * per_unit : (u + 1) * per_unit]:
            copy.wait()
        for first, count, out_first in jobs[u]:

            def step(j, carry, u=u, first=first, out_first=out_first, waited=waited):
                @pl.when(first + j >= waited)
                def _():
                    for seq in range(2):
                        pltpu.make_async_copy(
                            act_refs[0][seq].at[:, :, pl.ds(0, QUARTER)],
                            values.at[first + j, seq],
                            value_sem.at[first + j, seq],
                        ).wait()

                act = values[first + j].reshape(-1, QUARTER)
                tile = jnp.dot(grads[u], act, preferred_element_type=jnp.float32)
                at = out_first + j
                results[at] = tile.astype(results.dtype)
                for part in range(NZ):
                    pltpu.make_async_copy(
                        results.at[at, pl.ds(part * ROWS, ROWS), :],
                        outs[part].at[:, pl.ds(pl.multiple_of(at * QUARTER, QUARTER), QUARTER)],
                        result_sem.at[at, part],
                    ).start()
                return carry

            lax.fori_loop(0, count, step, 0)
            waited = max(waited, first + count)
            done += count

    def settle(at, carry):
        for part in range(NZ):
            pltpu.make_async_copy(
                results.at[at, pl.ds(part * ROWS, ROWS), :],
                outs[part].at[:, pl.ds(pl.multiple_of(at * QUARTER, QUARTER), QUARTER)],
                result_sem.at[at, part],
            ).wait()
        return carry

    lax.fori_loop(0, done, settle, 0)


def products(pieces, acts, jobs):
    units, count = len(pieces), 2 * len(acts)
    total = sum(n for runs in jobs for _, n, _ in runs)
    operands = [a for piece in pieces for a in piece] + [a for pair in acts for a in pair]
    tokens = pieces[0][0].shape[-1]
    shape = acts[0][0].shape[:2] + (QUARTER,)
    flops = 2 * total * QUARTER * NZ * ROWS * 2 * shape[0] * shape[1]
    return pl.pallas_call(
        functools.partial(product_kernel, jobs=jobs, units=units, acts=count),
        in_specs=[pl.BlockSpec(memory_space=pl.ANY)] * len(operands),
        out_specs=[pl.BlockSpec(memory_space=pl.ANY)] * NZ,
        out_shape=[jax.ShapeDtypeStruct((ROWS, total * QUARTER), jnp.bfloat16)] * NZ,
        scratch_shapes=[
            pltpu.VMEM((units, NZ * ROWS, 4 * NX * tokens), jnp.bfloat16),
            pltpu.VMEM((count, 2) + shape, jnp.bfloat16),
            pltpu.VMEM((total, NZ * ROWS, QUARTER), jnp.bfloat16),
            pltpu.SemaphoreType.DMA((units, 4 * NX)),
            pltpu.SemaphoreType.DMA((count, 2)),
            pltpu.SemaphoreType.DMA((total, NZ)),
        ],
        cost_estimate=pl.CostEstimate(flops=flops, bytes_accessed=2**20, transcendentals=0),
    )(*operands)


def reduce_over_z(parts, upward, hold):
    f32 = jnp.float32
    far, up, down, own = parts
    passing = send(far, Z_UP if upward else Z_DOWN)
    if hold is not None:
        passing, _ = lax.optimization_barrier((passing, hold))
    if upward:
        below_sent = send((up.astype(f32) + passing.astype(f32)).astype(up.dtype), Z_UP)
        above_sent = send(down, Z_DOWN)
    else:
        above_sent = send((down.astype(f32) + passing.astype(f32)).astype(down.dtype), Z_DOWN)
        below_sent = send(up, Z_UP)
    return own, below_sent, above_sent


HEADS_PER_HALF = 2 * QUARTER // HEAD_DIM

PORTIONS = (
    ("pa", ((0, "own", 0, 4),)),
    ("pb", ((0, "y", 0, 2), (1, "own", 0, 4), (1, "y", 0, 2))),
    ("pc", ((0, "y", 2, 2), (1, "y", 2, 2))),
    ("pd", ((2, "own", 0, 4), (2, "y", 0, 4))),
    ("pe", ((3, "own", 0, 4), (3, "y", 0, 4))),
)
OUTER = (("pa", "pb", "pc"), ("pd",))


def program(saved_queries, saved_keys, saved_values, out_grad, act_exponent, grad_exponent):
    f32, bf16 = jnp.float32, jnp.bfloat16
    yh, _, c, yl, _ = position()
    chip = yl ^ yh
    dequant = jnp.exp2((act_exponent[0] + grad_exponent[0]).astype(f32)) / (SATURATION * SATURATION)

    blocks = quantize_columns(grad_exponent, out_grad, FIRST)
    blocks |= quantize_columns(grad_exponent, out_grad, REST)
    near_sent = [send(blocks[1, 0, *group], CORES) for group in ((0, 1), (1, 3))]
    theirs = [near_sent[0][0], *(near_sent[1][i] for i in range(3))]
    mine = [blocks[0, 0, unit, 1][0] for unit in range(UNITS)]

    acts = {}
    for half in range(2):
        a = attend(act_exponent, saved_queries, saved_keys, saved_values, half * HEADS_PER_HALF, HEADS_PER_HALF)
        acts["own", half] = (a, send(a, CORES))
        b = send(a, Y_INNER)
        acts["y", half] = (b, send(b, CORES))

    from_y = {}
    for first, count in GROUPS:
        near = send(blocks[0, 1, first, count], Y_INNER)
        other = send(send(blocks[1, 1, first, count], CORES), Y_INNER)
        if count > 1:
            near, other, _ = lax.optimization_barrier((near, other, acts["own", 1][0]))
        for unit in range(first, first + count):
            from_y[unit] = (near[unit - first], other[unit - first])

    pieces = []
    for unit in range(UNITS):
        block = jnp.stack([mine[unit], from_y[unit][0], theirs[unit], from_y[unit][1]])
        block = block.reshape((2, 2) + block.shape[1:])
        left = send(block, X_UP)
        right = send(block, X_DOWN)
        far = send(left, X_UP) if unit % 2 == 0 else send(right, X_DOWN)
        pieces.append((block, left, right, far))

    made = {}
    for name, runs in PORTIONS:
        units, used, jobs, at = [], [], [], 0
        for unit, side, first, count in runs:
            if unit not in units:
                units.append(unit)
                jobs.append([])
            for quarter in range(first, first + count):
                if (side, quarter) not in used:
                    used.append((side, quarter))
            jobs[units.index(unit)].append((used.index((side, first)), count, at))
            at += count
        halves = [acts[side, quarter // 2] for side, quarter in used[::2]]
        made[name] = products([pieces[u] for u in units], halves, jobs)

    sums = {}
    leaving = {}
    for index, (name, runs) in enumerate(PORTIONS):
        later = made[PORTIONS[index + 1][0]][3] if index + 1 < len(PORTIONS) else None
        own, below, above = reduce_over_z(made[name], index % 2 == 0, later)
        at = 0
        leaving[name] = []
        for unit, side, first, count in runs:
            for k in range(count):
                sums[unit, side, first + k] = (own, below, above, at)
                if unit % 2 == 0:
                    leaving[name].append((unit, side, first + k))
                at += 1

    outgoing, out_places = {}, []
    for index, names in enumerate(OUTER):
        at, columns = 0, []
        for name in names:
            cut = len(leaving[name]) * QUARTER
            own, below, above, _ = sums[leaving[name][0]]
            if index == 0:
                own, below, above, _ = lax.optimization_barrier((own, below, above, made["pe"][3]))
            columns.append(own[:, :cut].astype(f32) + below[:, :cut].astype(f32) + above[:, :cut].astype(f32))
            for key in leaving[name]:
                out_places.append((*key, index, at))
                at += 1
        message = jnp.concatenate(columns, 1).astype(bf16)
        outgoing[index] = send(message, Y_OUTER)
        if index:
            outgoing[0], _ = lax.optimization_barrier((outgoing[0], message))

    incoming = {}
    for unit, side, quarter, name, at in out_places:
        incoming[unit + 1, "y" if side == "own" else "own", quarter] = (outgoing[name], at)

    def total(unit, side, hold=None):
        columns = []
        for quarter in range(4):
            own, below, above, at = sums[unit, side, quarter]
            arrived, there = incoming[unit, side, quarter]
            if hold is not None:
                own, below, above, arrived, _ = lax.optimization_barrier((own, below, above, arrived, hold))
            cut = slice(at * QUARTER, (at + 1) * QUARTER)
            columns.append(
                own[:, cut].astype(f32)
                + below[:, cut].astype(f32)
                + above[:, cut].astype(f32)
                + arrived[:, there * QUARTER : (there + 1) * QUARTER].astype(f32)
            )
        return jnp.concatenate(columns, 1)

    keeps, gifts = [], []
    for half in range(2):
        unit = 2 * half + 1
        leaves = total(unit, "y").astype(bf16)
        swapped = send(leaves, Y_INNER)
        near = total(unit, "own", leaves)
        stays = chip == c
        keeps.append(jnp.where(stays, near, swapped.astype(f32)))
        gifts.append(send(jnp.where(stays, swapped, near.astype(bf16)), CORES).astype(f32))
    keep, gift = jnp.concatenate(keeps, 0), jnp.concatenate(gifts, 0)
    result = jnp.where(c == 0, jnp.stack([keep, gift]), jnp.stack([gift, keep])) * dequant
    return result.reshape(4 * ROWS, -1)


def solution(mesh):
    in_specs = (
        P("dp", "tensor"),
        P("dp", "tensor"),
        P("dp", "tensor"),
        P(("dp", "tensor"), None),
        P(),
        P(),
    )
    out_specs = P("dp", "tensor")
    return jax.shard_map(program, mesh=mesh, in_specs=in_specs, out_specs=out_specs, check_vma=False)
```

profile of v0, /device:TPU:0, one launch (start us, length us, event | category | flops | bytes accessed | tf_op | source)
XLA Modules:
  0.0 246.9 jit_solution(771710348074685650)
XLA Ops:
  0.7 2.6 %shard_map.64 = (bf16[1,512,128]{2,1,0:T(8,128)(2,1)}, bf16[1,512,128]{2,1,0:T(8,128)(2,1)}, bf16[1,512,128]{2,1,0:T(8,128)(2,1)}, bf16[1,512,128]{2,1,0:T(8,128)(2,1)}) custom-call(s32[1]{0:T(128)S(6)} %copy.8.exponent_ref, bf16[128,8192]{1,0:T(8,128)(2,1)} %grad_ref.3), custom_call_target="tpu_custom_call" | custom-call | flops 2000000000 | bytes 3145728 | tf_op jit(solution)/shard_map/pallas_call | solution.py:83
  3.2 3.2 %shard_map.65 = (bf16[3,512,128]{2,1,0:T(8,128)(2,1)}, bf16[1,512,128]{2,1,0:T(8,128)(2,1)}, bf16[2,512,128]{2,1,0:T(8,128)(2,1)}, bf16[1,512,128]{2,1,0:T(8,128...) custom-call(s32[1]{0:T(128)S(6)} %copy.8.exponent_ref, ...), custom_call_target="tpu_custom_call" | custom-call | flops 2000000000 | bytes 3145728 | tf_op jit(solution)/shard_map/pallas_call | solution.py:83
  10.0 9.0 %shard_map.67.refs_12_.refs_6_ = bf16[8,128,512]{2,1,0:T(8,128)(2,1)} custom-call(s32[1]{0:T(128)S(6)} %copy.7.exponent_ref, bf16[1024,1024]{1,0:T(8,128)(2,1)} %query_ref.3, bf16[1024,128]{1,0:T(8,128)(2,1)} %key_ref.3, bf16[1024,128]{1,0:T(8,128)(2,1)} %value_ref.3), custom_call_target="tpu_custom_call" | custom-call | flops 4000000000 | bytes 1048576 | tf_op jit(solution)/shard_map/pallas_call | solution.py:139
  19.0 1.8 collective-permute-start.26
  21.3 1.8 collective-permute-start.7
  23.4 30.1 %collective-permute-done.7 = bf16[1,512,128]{2,1,0:T(8,128)(2,1)S(1)} collective-permute-done((bf16[1,512,128]{2,1,0:T(8,128)(2,1)S(1)}, bf16[1,512,128]{2,1,0:T(8,128)(2,1)S(1)}, u32[]{:S(2)}, u32[]{:S(2)}) %collective-permute-start.7) | collective-permute-done | bytes 131104 | tf_op jit(solution)/shard_map/ppermute | solution.py:46
  58.9 9.1 %shard_map.66.refs_10_.refs_4_ = bf16[8,128,512]{2,1,0:T(8,128)(2,1)} custom-call(s32[1]{0:T(128)S(6)} %copy.7.exponent_ref, bf16[1024,1024]{1,0:T(8,128)(2,1)} %query_ref.3, bf16[1024,128]{1,0:T(8,128)(2,1)} %key_ref.3, bf16[1024,128]{1,0:T(8,128)(2,1)} %value_ref.3), custom_call_target="tpu_custom_call" | custom-call | flops 4000000000 | bytes 1048576 | tf_op jit(solution)/shard_map/pallas_call | solution.py:139
  70.1 8.2 %collective-permute-done.11.refs_5_ = bf16[2,2,512,128]{3,2,1,0:T(8,128)(2,1)} collective-permute-done((bf16[2,2,512,128]{3,2,1,0:T(8,128)(2,1)S(1)}, bf16[2,2,512,128]{3,2,1,0:T(8,128)(2,1)}, u32[]{:S(2)}, u32[]{:S(2)}) %collective-permute-start.11) | collective-permute-done | bytes 524320 | tf_op jit(solution)/shard_map/ppermute | solution.py:46
  79.9 10.1 %collective-permute-done.12.refs_6_ = bf16[2,2,512,128]{3,2,1,0:T(8,128)(2,1)} collective-permute-done((bf16[2,2,512,128]{3,2,1,0:T(8,128)(2,1)S(1)}, bf16[2,2,512,128]{3,2,1,0:T(8,128)(2,1)}, u32[]{:S(2)}, u32[]{:S(2)}) %collective-permute-start.12) | collective-permute-done | bytes 524320 | tf_op jit(solution)/shard_map/ppermute | solution.py:46
  90.1 1.7 collective-permute-done.14.refs_8_
  96.4 9.8 %collective-permute-done.6.refs_3_ = bf16[2,2,512,128]{3,2,1,0:T(8,128)(2,1)} collective-permute-done((bf16[2,2,512,128]{3,2,1,0:T(8,128)(2,1)}, bf16[2,2,512,128]{3,2,1,0:T(8,128)(2,1)}, u32[]{:S(2)}, u32[]{:S(2)}) %collective-permute-start.6) | collective-permute-done | bytes 524320 | tf_op jit(solution)/shard_map/ppermute | solution.py:46
  107.6 6.7 %shard_map.70 = (bf16[128,1024]{1,0:T(8,128)(2,1)}, bf16[128,1024]{1,0:T(8,128)(2,1)}, bf16[128,1024]{1,0:T(8,128)(2,1)}, bf16[128,1024]{1,0:T(8,128)(2,1)}) custom-call(bf16[2,2,512,128]{3,2,1,0:T(8,128)(2,1)} %bitcast.15, bf16[2,2,512,128]{3,2,1,0:T(8,128)(2,1)} %collective-permute-done.4.refs_1_, bf16[2,2,512,128]{3,2,1,0:T(8,128)(2,1)} %collective-permute-done.5.refs_2_, ...), custom_call_target="tpu_custom_call" | custom-call | flops 2147483648 | bytes 1048576 | tf_op jit(solution)/shard_map/pallas_call | solution.py:235
  116.4 4.8 %collective-permute-done.13.refs_7_ = bf16[2,2,512,128]{3,2,1,0:T(8,128)(2,1)S(1)} collective-permute-done((bf16[2,2,512,128]{3,2,1,0:T(8,128)(2,1)}, bf16[2,2,512,128]{3,2,1,0:T(8,128)(2,1)S(1)}, u32[]{:S(2)}, u32[]{:S(2)}) %collective-permute-start.13) | collective-permute-done | bytes 524320 | tf_op jit(solution)/shard_map/ppermute | solution.py:46
  122.0 2.5 %collective-permute-start.31 = (bf16[2,2,512,128]{3,2,1,0:T(8,128)(2,1)}, bf16[2,2,512,128]{3,2,1,0:T(8,128)(2,1)}, u32[]{:S(2)}, u32[]{:S(2)}) collective-permute-start(bf16[2,2,512,128]{3,2,1,0:T(8,128)(2,1)} %collective-permute-done.30.refs_2_), channel_id=1, source_target_pairs={{0,3},{1,0},{2,1},{3,2},{4,7},{5,4},{6,5},{7,6},{8,11},{9,8},{10,9... | collective-permute-start | bytes 1572872 | tf_op jit(solution)/shard_map/ppermute | solution.py:46
  124.5 6.6 %shard_map.69 = (bf16[128,1024]{1,0:T(8,128)(2,1)}, bf16[128,1024]{1,0:T(8,128)(2,1)}, bf16[128,1024]{1,0:T(8,128)(2,1)}, bf16[128,1024]{1,0:T(8,128)(2,1)}) custom-call(bf16[2,2,512,128]{3,2,1,0:T(8,128)(2,1)} %bitcast.16, bf16[2,2,512,128]{3,2,1,0:T(8,128)(2,1)} %collective-permute-done.4.refs_1_, bf16[2,2,512,128]{3,2,1,0:T(8,128)(2,1)} %collective-permute-done.5.refs_2_, ...), custom_call_target="tpu_custom_call" | custom-call | flops 2147483648 | bytes 1048576 | tf_op jit(solution)/shard_map/pallas_call | solution.py:235
  131.1 1.8 collective-permute-start.23
  132.9 9.8 %shard_map.68 = (bf16[128,2048]{1,0:T(8,128)(2,1)}, bf16[128,2048]{1,0:T(8,128)(2,1)}, bf16[128,2048]{1,0:T(8,128)(2,1)}, bf16[128,2048]{1,0:T(8,128)(2,1)}) custom-call(bf16[2,2,512,128]{3,2,1,0:T(8,128)(2,1)} %bitcast.17, bf16[2,2,512,128]{3,2,1,0:T(8,128)(2,1)} %collective-permute-done.4.refs_1_, bf16[2,2,512,128]{3,2,1,0:T(8,128)(2,1)} %collective-permute-done.5.refs_2_, ...), custom_call_target="tpu_custom_call" | custom-call | flops 4294967296 | bytes 1048576 | tf_op jit(solution)/shard_map/pallas_call | solution.py:235
  142.8 2.2 collective-permute-start.25
  145.8 10.8 %shard_map.72 = (bf16[128,2048]{1,0:T(8,128)(2,1)}, bf16[128,2048]{1,0:T(8,128)(2,1)}, bf16[128,2048]{1,0:T(8,128)(2,1)}, bf16[128,2048]{1,0:T(8,128)(2,1)}) custom-call(bf16[2,2,512,128]{3,2,1,0:T(8,128)(2,1)} %bitcast.27, bf16[2,2,512,128]{3,2,1,0:T(8,128)(2,1)} %copy-done.28, bf16[2,2,512,128]{3,2,1,0:T(8,128)(2,1)} %copy-done.29, ...), custom_call_target="tpu_custom_call" | custom-call | flops 4294967296 | bytes 1048576 | tf_op jit(solution)/shard_map/pallas_call | solution.py:235
  156.7 2.6 %collective-permute-start.40 = (bf16[128,2048]{1,0:T(8,128)(2,1)}, bf16[128,2048]{1,0:T(8,128)(2,1)S(1)}, u32[]{:S(2)}, u32[]{:S(2)}) collective-permute-start(bf16[128,2048]{1,0:T(8,128)(2,1)} %get-tuple-element.103), channel_id=1, source_target_pairs={{0,48},{1,49},{2,50},{3,51},{4,52},{5,53},{6,54},{7,55},{8,56},{9,... | collective-permute-start | bytes 1572872 | tf_op jit(solution)/shard_map/ppermute | solution.py:46
  161.7 10.9 %shard_map.71 = (bf16[128,2048]{1,0:T(8,128)(2,1)}, bf16[128,2048]{1,0:T(8,128)(2,1)}, bf16[128,2048]{1,0:T(8,128)(2,1)}, bf16[128,2048]{1,0:T(8,128)(2,1)}) custom-call(bf16[2,2,512,128]{3,2,1,0:T(8,128)(2,1)} %bitcast.24, bf16[2,2,512,128]{3,2,1,0:T(8,128)(2,1)} %collective-permute-done.29.refs_1_, ...), custom_call_target="tpu_custom_call" | custom-call | flops 4294967296 | bytes 1048576 | tf_op jit(solution)/shard_map/pallas_call | solution.py:235
  174.5 2.8 %collective-permute-start.45 = (bf16[128,2048]{1,0:T(8,128)(2,1)}, bf16[128,2048]{1,0:T(8,128)(2,1)S(1)}, u32[]{:S(2)}, u32[]{:S(2)}) collective-permute-start(bf16[128,2048]{1,0:T(8,128)(2,1)} %get-tuple-element.112), channel_id=1, source_target_pairs={{0,48},{1,49},{2,50},{3,51},{4,52},{5,53},{6,54},{7,55},{8,56},{9,... | collective-permute-start | bytes 1572872 | tf_op jit(solution)/shard_map/ppermute | solution.py:46
  178.9 3.2 %collective-permute-start.19 = (bf16[128,2048]{1,0:T(8,128)(2,1)}, bf16[128,2048]{1,0:T(8,128)(2,1)S(1)}, u32[]{:S(2)}, u32[]{:S(2)}) collective-permute-start(bf16[128,2048]{1,0:T(8,128)(2,1)} %get-tuple-element.72), channel_id=1, source_target_pairs={{0,48},{1,49},{2,50},{3,51},{4,52},{5,53},{6,54},{7,55},{8,56},{9,... | collective-permute-start | bytes 1572872 | tf_op jit(solution)/shard_map/ppermute | solution.py:46
  182.4 16.4 %collective-permute-done.19 = bf16[128,2048]{1,0:T(8,128)(2,1)S(1)} collective-permute-done((bf16[128,2048]{1,0:T(8,128)(2,1)}, bf16[128,2048]{1,0:T(8,128)(2,1)S(1)}, u32[]{:S(2)}, u32[]{:S(2)}) %collective-permute-start.19) | collective-permute-done | bytes 524320 | tf_op jit(solution)/shard_map/ppermute | solution.py:46
  198.8 2.1 collective-permute-start.41
  201.0 1.9 collective-permute-start.22
  203.3 10.0 %collective-permute-done.41 = bf16[128,2048]{1,0:T(8,128)(2,1)S(1)} collective-permute-done((bf16[128,2048]{1,0:T(8,128)(2,1)S(1)}, bf16[128,2048]{1,0:T(8,128)(2,1)S(1)}, u32[]{:S(2)}, u32[]{:S(2)}) %collective-permute-start.41) | collective-permute-done | bytes 524320 | tf_op jit(solution)/shard_map/ppermute | solution.py:46
  215.7 3.2 %collective-permute-done.22 = bf16[128,2048]{1,0:T(8,128)(2,1)S(1)} collective-permute-done((bf16[128,2048]{1,0:T(8,128)(2,1)S(1)}, bf16[128,2048]{1,0:T(8,128)(2,1)S(1)}, u32[]{:S(2)}, u32[]{:S(2)}) %collective-permute-start.22) | collective-permute-done | bytes 524320 | tf_op jit(solution)/shard_map/ppermute | solution.py:46
  222.3 7.9 %collective-permute-done.46 = bf16[128,2048]{1,0:T(8,128)(2,1)S(1)} collective-permute-done((bf16[128,2048]{1,0:T(8,128)(2,1)}, bf16[128,2048]{1,0:T(8,128)(2,1)S(1)}, u32[]{:S(2)}, u32[]{:S(2)}) %collective-permute-start.46) | collective-permute-done | bytes 524320 | tf_op jit(solution)/shard_map/ppermute | solution.py:46
  230.5 5.3 %collective-permute-done.38 = bf16[128,2048]{1,0:T(8,128)(2,1)S(1)} collective-permute-done((bf16[128,2048]{1,0:T(8,128)(2,1)}, bf16[128,2048]{1,0:T(8,128)(2,1)S(1)}, u32[]{:S(2)}, u32[]{:S(2)}) %collective-permute-start.38) | collective-permute-done | bytes 524320 | tf_op jit(solution)/shard_map/ppermute | solution.py:46
  237.5 2.1 collective-permute-done.47
  239.7 3.8 %collective-permute-done.42 = bf16[128,1024]{1,0:T(8,128)(2,1)S(1)} collective-permute-done((bf16[128,1024]{1,0:T(8,128)(2,1)S(1)}, bf16[128,1024]{1,0:T(8,128)(2,1)S(1)}, u32[]{:S(2)}, u32[]{:S(2)}) %collective-permute-start.42) | collective-permute-done | bytes 262176 | tf_op jit(solution)/shard_map/ppermute | solution.py:46
  (180 shorter events, 40.1 us)
Async XLA Ops:
  6.5 16.6 %collective-permute-start.8 = (bf16[3,512,128]{2,1,0:T(8,128)(2,1)}, bf16[3,512,128]{2,1,0:T(8,128)(2,1)S(1)}, u32[]{:S(2)}, u32[]{:S(2)}) collective-permute-start(bf16[3,512,128]{2,1,0:T(8,128)(2,1)} %get-tuple-element.67), channel_id=1, source_target_pairs={{0,8},{1,9},{2,10},{3,11},{4,12},{5,13},{6,14},{7,15},{8,0},{9,1},... | collective-permute-start | bytes 1179656 | tf_op jit(solution)/shard_map/ppermute | solution.py:46
  19.0 39.6 %collective-permute-start.26 = (bf16[2,512,128]{2,1,0:T(8,128)(2,1)S(1)}, bf16[2,512,128]{2,1,0:T(8,128)(2,1)S(1)}, u32[]{:S(2)}, u32[]{:S(2)}) collective-permute-start(bf16[2,512,128]{2,1,0:T(8,128)(2,1)S(1)} %copy-done.32), channel_id=1, source_target_pairs={{0,4},{1,5},{2,6},{3,7},{4,0},{5,1},{6,2},{7,3},{8,12},{9,13},{10,... | collective-permute-start | bytes 786440 | tf_op jit(solution)/shard_map/ppermute | solution.py:46
  20.7 34.4 %collective-permute-start.27 = (bf16[2,512,128]{2,1,0:T(8,128)(2,1)S(1)}, bf16[2,512,128]{2,1,0:T(8,128)(2,1)}, u32[]{:S(2)}, u32[]{:S(2)}) collective-permute-start(bf16[2,512,128]{2,1,0:T(8,128)(2,1)S(1)} %copy-done.33), channel_id=1, source_target_pairs={{0,8},{1,9},{2,10},{3,11},{4,12},{5,13},{6,14},{7,15},{8,0},{9,1},... | collective-permute-start | bytes 786440 | tf_op jit(solution)/shard_map/ppermute | solution.py:46
  20.8 69.3 %collective-permute-start.20 = (bf16[8,128,512]{2,1,0:T(8,128)(2,1)}, bf16[8,128,512]{2,1,0:T(8,128)(2,1)}, u32[]{:S(2)}, u32[]{:S(2)}) collective-permute-start(bf16[8,128,512]{2,1,0:T(8,128)(2,1)} %shard_map.67.refs_12_.refs_6_), channel_id=1, source_target_pairs={{0,4},{1,5},{2,6},{3,7},{4,0},{5,1},{6,2},{7,3},{8,12},{9,13},{10,... | collective-permute-start | bytes 3145736 | tf_op jit(solution)/shard_map/ppermute | solution.py:46
  21.3 32.2 %collective-permute-start.7 = (bf16[1,512,128]{2,1,0:T(8,128)(2,1)S(1)}, bf16[1,512,128]{2,1,0:T(8,128)(2,1)S(1)}, u32[]{:S(2)}, u32[]{:S(2)}) collective-permute-start(bf16[1,512,128]{2,1,0:T(8,128)(2,1)S(1)} %copy-done.34), channel_id=1, source_target_pairs={{0,4},{1,5},{2,6},{3,7},{4,0},{5,1},{6,2},{7,3},{8,12},{9,13},{10,... | collective-permute-start | bytes 393224 | tf_op jit(solution)/shard_map/ppermute | solution.py:46
  23.1 33.7 %collective-permute-start.10 = (bf16[1,512,128]{2,1,0:T(8,128)(2,1)S(1)}, bf16[1,512,128]{2,1,0:T(8,128)(2,1)S(1)}, u32[]{:S(2)}, u32[]{:S(2)}) collective-permute-start(bf16[1,512,128]{2,1,0:T(8,128)(2,1)S(1)} %collective-permute-done.9), channel_id=1, source_target_pairs={{0,4},{1,5},{2,6},{3,7},{4,0},{5,1},{6,2},{7,3},{8,12},{9,13},{10,... | collective-permute-start | bytes 393224 | tf_op jit(solution)/shard_map/ppermute | solution.py:46
  53.5 16.1 %collective-permute-start.4 = (bf16[2,2,512,128]{3,2,1,0:T(8,128)(2,1)S(1)}, bf16[2,2,512,128]{3,2,1,0:T(8,128)(2,1)}, u32[]{:S(2)}, u32[]{:S(2)}) collective-permute-start(bf16[2,2,512,128]{3,2,1,0:T(8,128)(2,1)S(1)} %bitcast.13), channel_id=1, source_target_pairs={{0,1},{1,2},{2,3},{3,0},{4,5},{5,6},{6,7},{7,4},{8,9},{9,10},{10,1... | collective-permute-start | bytes 1572872 | tf_op jit(solution)/shard_map/ppermute | solution.py:46
  58.6 19.8 %collective-permute-start.11 = (bf16[2,2,512,128]{3,2,1,0:T(8,128)(2,1)S(1)}, bf16[2,2,512,128]{3,2,1,0:T(8,128)(2,1)}, u32[]{:S(2)}, u32[]{:S(2)}) collective-permute-start(bf16[2,2,512,128]{3,2,1,0:T(8,128)(2,1)S(1)} %bitcast.18), channel_id=1, source_target_pairs={{0,1},{1,2},{2,3},{3,0},{4,5},{5,6},{6,7},{7,4},{8,9},{9,10},{10,1... | collective-permute-start | bytes 1572872 | tf_op jit(solution)/shard_map/ppermute | solution.py:46
  68.0 23.8 %collective-permute-start.14 = (bf16[8,128,512]{2,1,0:T(8,128)(2,1)}, bf16[8,128,512]{2,1,0:T(8,128)(2,1)}, u32[]{:S(2)}, u32[]{:S(2)}) collective-permute-start(bf16[8,128,512]{2,1,0:T(8,128)(2,1)} %shard_map.66.refs_10_.refs_4_), channel_id=1, source_target_pairs={{0,4},{1,5},{2,6},{3,7},{4,0},{5,1},{6,2},{7,3},{8,12},{9,13},{10,... | collective-permute-start | bytes 3145736 | tf_op jit(solution)/shard_map/ppermute | solution.py:46
  69.6 22.4 %collective-permute-start.16 = (bf16[8,128,512]{2,1,0:T(8,128)(2,1)}, bf16[8,128,512]{2,1,0:T(8,128)(2,1)S(1)}, u32[]{:S(2)}, u32[]{:S(2)}) collective-permute-start(bf16[8,128,512]{2,1,0:T(8,128)(2,1)} %shard_map.66.refs_10_.refs_4_), channel_id=1, source_target_pairs={{0,8},{1,9},{2,10},{3,11},{4,12},{5,13},{6,14},{7,15},{8,0},{9,1},... | collective-permute-start | bytes 3145736 | tf_op jit(solution)/shard_map/ppermute | solution.py:46
  69.6 24.0 %collective-permute-start.17 = (bf16[8,128,512]{2,1,0:T(8,128)(2,1)S(1)}, bf16[8,128,512]{2,1,0:T(8,128)(2,1)S(1)}, u32[]{:S(2)}, u32[]{:S(2)}) collective-permute-start(bf16[8,128,512]{2,1,0:T(8,128)(2,1)S(1)} %copy-done.25), channel_id=1, source_target_pairs={{0,8},{1,9},{2,10},{3,11},{4,12},{5,13},{6,14},{7,15},{8,0},{9,1},... | collective-permute-start | bytes 3145736 | tf_op jit(solution)/shard_map/ppermute | solution.py:46
  89.9 16.3 %collective-permute-start.6 = (bf16[2,2,512,128]{3,2,1,0:T(8,128)(2,1)}, bf16[2,2,512,128]{3,2,1,0:T(8,128)(2,1)}, u32[]{:S(2)}, u32[]{:S(2)}) collective-permute-start(bf16[2,2,512,128]{3,2,1,0:T(8,128)(2,1)} %collective-permute-done.4.refs_1_), channel_id=1, source_target_pairs={{0,1},{1,2},{2,3},{3,0},{4,5},{5,6},{6,7},{7,4},{8,9},{9,10},{10,1... | collective-permute-start | bytes 1572872 | tf_op jit(solution)/shard_map/ppermute | solution.py:46
  90.1 31.9 %collective-permute-start.21 = (bf16[8,128,512]{2,1,0:T(8,128)(2,1)}, bf16[8,128,512]{2,1,0:T(8,128)(2,1)}, u32[]{:S(2)}, u32[]{:S(2)}) collective-permute-start(bf16[8,128,512]{2,1,0:T(8,128)(2,1)} %collective-permute-done.20.refs_8_.refs_10_), channel_id=1, source_target_pairs={{0,8},{1,9},{2,10},{3,11},{4,12},{5,13},{6,14},{7,15},{8,0},{9,1},... | collective-permute-start | bytes 3145736 | tf_op jit(solution)/shard_map/ppermute | solution.py:46
  91.8 39.3 %collective-permute-start.15 = (bf16[8,128,512]{2,1,0:T(8,128)(2,1)}, bf16[8,128,512]{2,1,0:T(8,128)(2,1)}, u32[]{:S(2)}, u32[]{:S(2)}) collective-permute-start(bf16[8,128,512]{2,1,0:T(8,128)(2,1)} %collective-permute-done.14.refs_8_), channel_id=1, source_target_pairs={{0,8},{1,9},{2,10},{3,11},{4,12},{5,13},{6,14},{7,15},{8,0},{9,1},... | collective-permute-start | bytes 3145736 | tf_op jit(solution)/shard_map/ppermute | solution.py:46
  92.1 22.2 %collective-permute-start.33 = (bf16[2,2,512,128]{3,2,1,0:T(8,128)(2,1)S(1)}, bf16[2,2,512,128]{3,2,1,0:T(8,128)(2,1)S(1)}, u32[]{:S(2)}, u32[]{:S(2)}) collective-permute-start(bf16[2,2,512,128]{3,2,1,0:T(8,128)(2,1)S(1)} %bitcast.25), channel_id=1, source_target_pairs={{0,1},{1,2},{2,3},{3,0},{4,5},{5,6},{6,7},{7,4},{8,9},{9,10},{10,1... | collective-permute-start | bytes 1572872 | tf_op jit(solution)/shard_map/ppermute | solution.py:46
  94.7 20.2 %collective-permute-start.30 = (bf16[2,2,512,128]{3,2,1,0:T(8,128)(2,1)S(1)}, bf16[2,2,512,128]{3,2,1,0:T(8,128)(2,1)}, u32[]{:S(2)}, u32[]{:S(2)}) collective-permute-start(bf16[2,2,512,128]{3,2,1,0:T(8,128)(2,1)S(1)} %bitcast.22), channel_id=1, source_target_pairs={{0,3},{1,0},{2,1},{3,2},{4,7},{5,4},{6,5},{7,6},{8,11},{9,8},{10,9... | collective-permute-start | bytes 1572872 | tf_op jit(solution)/shard_map/ppermute | solution.py:46
  114.3 28.5 %collective-permute-start.34 = (bf16[2,2,512,128]{3,2,1,0:T(8,128)(2,1)S(1)}, bf16[2,2,512,128]{3,2,1,0:T(8,128)(2,1)S(1)}, u32[]{:S(2)}, u32[]{:S(2)}) collective-permute-start(bf16[2,2,512,128]{3,2,1,0:T(8,128)(2,1)S(1)} %bitcast.26), channel_id=1, source_target_pairs={{0,3},{1,0},{2,1},{3,2},{4,7},{5,4},{6,5},{7,6},{8,11},{9,8},{10,9... | collective-permute-start | bytes 1572872 | tf_op jit(solution)/shard_map/ppermute | solution.py:46
  115.0 45.3 %collective-permute-start.29 = (bf16[2,2,512,128]{3,2,1,0:T(8,128)(2,1)S(1)}, bf16[2,2,512,128]{3,2,1,0:T(8,128)(2,1)}, u32[]{:S(2)}, u32[]{:S(2)}) collective-permute-start(bf16[2,2,512,128]{3,2,1,0:T(8,128)(2,1)S(1)} %bitcast.23), channel_id=1, source_target_pairs={{0,1},{1,2},{2,3},{3,0},{4,5},{5,6},{6,7},{7,4},{8,9},{9,10},{10,1... | collective-permute-start | bytes 1572872 | tf_op jit(solution)/shard_map/ppermute | solution.py:46
  121.3 23.8 %collective-permute-start.35 = (bf16[2,2,512,128]{3,2,1,0:T(8,128)(2,1)S(1)}, bf16[2,2,512,128]{3,2,1,0:T(8,128)(2,1)S(1)}, u32[]{:S(2)}, u32[]{:S(2)}) collective-permute-start(bf16[2,2,512,128]{3,2,1,0:T(8,128)(2,1)S(1)} %collective-permute-done.33.refs_1_), channel_id=1, source_target_pairs={{0,1},{1,2},{2,3},{3,0},{4,5},{5,6},{6,7},{7,4},{8,9},{9,10},{10,1... | collective-permute-start | bytes 1572872 | tf_op jit(solution)/shard_map/ppermute | solution.py:46
  122.0 39.7 %collective-permute-start.31 = (bf16[2,2,512,128]{3,2,1,0:T(8,128)(2,1)}, bf16[2,2,512,128]{3,2,1,0:T(8,128)(2,1)}, u32[]{:S(2)}, u32[]{:S(2)}) collective-permute-start(bf16[2,2,512,128]{3,2,1,0:T(8,128)(2,1)} %collective-permute-done.30.refs_2_), channel_id=1, source_target_pairs={{0,3},{1,0},{2,1},{3,2},{4,7},{5,4},{6,5},{7,6},{8,11},{9,8},{10,9... | collective-permute-start | bytes 1572872 | tf_op jit(solution)/shard_map/ppermute | solution.py:46
  131.1 25.6 %collective-permute-start.23 = (bf16[128,1024]{1,0:T(8,128)(2,1)}, bf16[128,1024]{1,0:T(8,128)(2,1)S(1)}, u32[]{:S(2)}, u32[]{:S(2)}) collective-permute-start(bf16[128,1024]{1,0:T(8,128)(2,1)} %get-tuple-element.77), channel_id=1, source_target_pairs={{0,16},{1,17},{2,18},{3,19},{4,20},{5,21},{6,22},{7,23},{8,24},{9,... | collective-permute-start | bytes 786440 | tf_op jit(solution)/shard_map/ppermute | solution.py:46
  142.8 29.8 %collective-permute-start.25 = (bf16[128,1024]{1,0:T(8,128)(2,1)}, bf16[128,1024]{1,0:T(8,128)(2,1)S(1)}, u32[]{:S(2)}, u32[]{:S(2)}) collective-permute-start(bf16[128,1024]{1,0:T(8,128)(2,1)} %get-tuple-element.79), channel_id=1, source_target_pairs={{0,48},{1,49},{2,50},{3,51},{4,52},{5,53},{6,54},{7,55},{8,56},{9,... | collective-permute-start | bytes 786440 | tf_op jit(solution)/shard_map/ppermute | solution.py:46
  156.7 25.5 %collective-permute-start.40 = (bf16[128,2048]{1,0:T(8,128)(2,1)}, bf16[128,2048]{1,0:T(8,128)(2,1)S(1)}, u32[]{:S(2)}, u32[]{:S(2)}) collective-permute-start(bf16[128,2048]{1,0:T(8,128)(2,1)} %get-tuple-element.103), channel_id=1, source_target_pairs={{0,48},{1,49},{2,50},{3,51},{4,52},{5,53},{6,54},{7,55},{8,56},{9,... | collective-permute-start | bytes 1572872 | tf_op jit(solution)/shard_map/ppermute | solution.py:46
  159.4 19.2 %collective-permute-start.37 = (bf16[128,1024]{1,0:T(8,128)(2,1)}, bf16[128,1024]{1,0:T(8,128)(2,1)S(1)}, u32[]{:S(2)}, u32[]{:S(2)}) collective-permute-start(bf16[128,1024]{1,0:T(8,128)(2,1)} %get-tuple-element.97), channel_id=1, source_target_pairs={{0,48},{1,49},{2,50},{3,51},{4,52},{5,53},{6,54},{7,55},{8,56},{9,... | collective-permute-start | bytes 786440 | tf_op jit(solution)/shard_map/ppermute | solution.py:46
  161.6 17.3 %collective-permute-start.36 = (bf16[128,1024]{1,0:T(8,128)(2,1)S(1)}, bf16[128,1024]{1,0:T(8,128)(2,1)S(1)}, u32[]{:S(2)}, u32[]{:S(2)}) collective-permute-start(bf16[128,1024]{1,0:T(8,128)(2,1)S(1)} %add_convert_fusion.4), channel_id=1, source_target_pairs={{0,16},{1,17},{2,18},{3,19},{4,20},{5,21},{6,22},{7,23},{8,24},{9,... | collective-permute-start | bytes 786440 | tf_op jit(solution)/shard_map/ppermute | solution.py:46
  173.3 29.7 %collective-permute-start.39 = (bf16[128,2048]{1,0:T(8,128)(2,1)}, bf16[128,2048]{1,0:T(8,128)(2,1)S(1)}, u32[]{:S(2)}, u32[]{:S(2)}) collective-permute-start(bf16[128,2048]{1,0:T(8,128)(2,1)} %get-tuple-element.101), channel_id=1, source_target_pairs={{0,16},{1,17},{2,18},{3,19},{4,20},{5,21},{6,22},{7,23},{8,24},{9,... | collective-permute-start | bytes 1572872 | tf_op jit(solution)/shard_map/ppermute | solution.py:46
  174.5 47.8 %collective-permute-start.45 = (bf16[128,2048]{1,0:T(8,128)(2,1)}, bf16[128,2048]{1,0:T(8,128)(2,1)S(1)}, u32[]{:S(2)}, u32[]{:S(2)}) collective-permute-start(bf16[128,2048]{1,0:T(8,128)(2,1)} %get-tuple-element.112), channel_id=1, source_target_pairs={{0,48},{1,49},{2,50},{3,51},{4,52},{5,53},{6,54},{7,55},{8,56},{9,... | collective-permute-start | bytes 1572872 | tf_op jit(solution)/shard_map/ppermute | solution.py:46
  178.5 22.4 %collective-permute-start.43 = (bf16[128,2048]{1,0:T(8,128)(2,1)}, bf16[128,2048]{1,0:T(8,128)(2,1)S(1)}, u32[]{:S(2)}, u32[]{:S(2)}) collective-permute-start(bf16[128,2048]{1,0:T(8,128)(2,1)} %get-tuple-element.111), channel_id=1, source_target_pairs={{0,16},{1,17},{2,18},{3,19},{4,20},{5,21},{6,22},{7,23},{8,24},{9,... | collective-permute-start | bytes 1572872 | tf_op jit(solution)/shard_map/ppermute | solution.py:46
  178.9 19.8 %collective-permute-start.19 = (bf16[128,2048]{1,0:T(8,128)(2,1)}, bf16[128,2048]{1,0:T(8,128)(2,1)S(1)}, u32[]{:S(2)}, u32[]{:S(2)}) collective-permute-start(bf16[128,2048]{1,0:T(8,128)(2,1)} %get-tuple-element.72), channel_id=1, source_target_pairs={{0,48},{1,49},{2,50},{3,51},{4,52},{5,53},{6,54},{7,55},{8,56},{9,... | collective-permute-start | bytes 1572872 | tf_op jit(solution)/shard_map/ppermute | solution.py:46
  182.2 33.6 %collective-permute-start.18 = (bf16[128,2048]{1,0:T(8,128)(2,1)}, bf16[128,2048]{1,0:T(8,128)(2,1)S(1)}, u32[]{:S(2)}, u32[]{:S(2)}) collective-permute-start(bf16[128,2048]{1,0:T(8,128)(2,1)} %get-tuple-element.70), channel_id=1, source_target_pairs={{0,16},{1,17},{2,18},{3,19},{4,20},{5,21},{6,22},{7,23},{8,24},{9,... | collective-permute-start | bytes 1572872 | tf_op jit(solution)/shard_map/ppermute | solution.py:46
  201.0 17.9 %collective-permute-start.22 = (bf16[128,2048]{1,0:T(8,128)(2,1)S(1)}, bf16[128,2048]{1,0:T(8,128)(2,1)S(1)}, u32[]{:S(2)}, u32[]{:S(2)}) collective-permute-start(bf16[128,2048]{1,0:T(8,128)(2,1)S(1)} %add_convert_fusion.3), channel_id=1, source_target_pairs={{0,48},{1,49},{2,50},{3,51},{4,52},{5,53},{6,54},{7,55},{8,56},{9,... | collective-permute-start | bytes 1572872 | tf_op jit(solution)/shard_map/ppermute | solution.py:46
  203.0 19.3 %collective-permute-start.44 = (bf16[128,2048]{1,0:T(8,128)(2,1)S(1)}, bf16[128,2048]{1,0:T(8,128)(2,1)S(1)}, u32[]{:S(2)}, u32[]{:S(2)}) collective-permute-start(bf16[128,2048]{1,0:T(8,128)(2,1)S(1)} %add_convert_fusion), channel_id=1, source_target_pairs={{0,16},{1,17},{2,18},{3,19},{4,20},{5,21},{6,22},{7,23},{8,24},{9,... | collective-permute-start | bytes 1572872 | tf_op jit(solution)/shard_map/ppermute | solution.py:46
  (55 other events, 772.5 us)
where the time goes:
time: 248 us; the launch traced here: 247 us
  waiting for transfers between devices  116 us (47%)
  Pallas kernels  68.6 us (28%)
  starting transfers between devices  48.1 us (19%)
  other arithmetic  8.62 us (3%)
  local copies, waits for them, and re-layouts  3.39 us (1%)
    ppermute x50, waiting for transfers between devices, send(): return lax.ppermute(block, AXES, pairs)  116 us
    ppermute x50, starting transfers between devices, send(): return lax.ppermute(block, AXES, pairs)  48.1 us
    pallas_call x5, Pallas kernels, products(): pl.pallas_call(functools.partial(product_kernel, jobs=jobs, units=units,...  44.8 us
    pallas_call x2, Pallas kernels, attend(): pl.pallas_call(attention_kernel, grid=(heads,), in_specs=[pl.BlockSpec(me...  18 us
    pallas_call x2, Pallas kernels, quantize_columns(): pl.pallas_call(functools.partial(quantize_kernel, made=made), in_specs=[p...  5.8 us
  transfers between devices with their start and end apart: 50, of which 15 were waited for; matrix products, arithmetic and copies ran while one was open for 3% of the time, Pallas kernels for 27%

commit v1 on v0

--- a/solution.py
+++ b/solution.py
@@ -16,6 +16,7 @@
 ROWS = 128
 STEPS = (2, 1, 3, 0)
 QUARTER = 256
+AHEAD = 2
 
 
 def device_of(yh, z, c, yl, x):
@@ -91,46 +92,60 @@
 
 
 Q_BLOCK = 256
+LOG2_E = 1.4426950408889634
 
 
 def attention_kernel(exponent_ref, query_ref, key_ref, value_ref, out_ref):
     _, _, _, _, x = position()
     seq_len = key_ref.shape[0]
-    scale = HEAD_DIM**-0.5
+    scale = HEAD_DIM**-0.5 * LOG2_E
     factor = saturation_factor(exponent_ref, HEAD_DIM)
     row = lax.broadcasted_iota(jnp.int32, (Q_BLOCK, Q_BLOCK), 0)
     column = lax.broadcasted_iota(jnp.int32, (Q_BLOCK, Q_BLOCK), 1)
     causal = column <= row
-    for start in range(0, seq_len, Q_BLOCK):
+
+    def scores_of(start):
         queries = query_ref[start : start + Q_BLOCK, :]
 
-        def scores_of(first, last):
+        def block(first, last):
             return lax.dot_general(
                 queries, key_ref[first:last, :], (((1,), (1,)), ((), ())), preferred_element_type=jnp.float32
             )
 
-        near = jnp.where(causal, scores_of(start, start + Q_BLOCK), jnp.float32(-1e30))
+        return block(start, start + Q_BLOCK), block(0, start) if start else None
+
+    def weights_of(near, past):
+        near = jnp.where(causal, near, jnp.float32(-1e30))
         row_max = jnp.max(near, axis=1, keepdims=True)
-        if start:
-            past = scores_of(0, start)
+        if past is not None:
             row_max = jnp.maximum(row_max, jnp.max(past, axis=1, keepdims=True))
-        weights = jnp.exp((near - row_max) * scale)
-        total = jnp.sum(weights, axis=1, keepdims=True)
-        mixed = jnp.dot(
-            weights.astype(jnp.bfloat16), value_ref[start : start + Q_BLOCK, :], preferred_element_type=jnp.float32
-        )
-        if start:
-            weights = jnp.exp((past - row_max) * scale)
-            total = total + jnp.sum(weights, axis=1, keepdims=True)
-            mixed = mixed + jnp.dot(
-                weights.astype(jnp.bfloat16), value_ref[:start, :], preferred_element_type=jnp.float32
-            )
+        near = jnp.exp2((near - row_max) * scale)
+        total = jnp.sum(near, axis=1, keepdims=True)
+        if past is not None:
+            past = jnp.exp2((past - row_max) * scale)
+            total = total + jnp.sum(past, axis=1, keepdims=True)
+            past = past.astype(jnp.bfloat16)
+        return near.astype(jnp.bfloat16), past, total
+
+    def finish(start, near, past, total):
+        mixed = jnp.dot(near, value_ref[start : start + Q_BLOCK, :], preferred_element_type=jnp.float32)
+        if past is not None:
+            mixed = mixed + jnp.dot(past, value_ref[:start, :], preferred_element_type=jnp.float32)
         scaled = jnp.clip(mixed / total * factor, -SATURATION, SATURATION).astype(jnp.bfloat16)
         for part in range(Q_BLOCK // ROWS):
             token_block = start // ROWS + part
             ahead = lax.rem(token_block % NX - x + NX, NX)
             order = jnp.where(ahead == 0, 0, jnp.where(ahead == 3, 1, ahead + 1))
             out_ref[pl.ds(order * 2 + token_block // NX, 1)] = scaled[part * ROWS : (part + 1) * ROWS][None]
+
+    scores, waiting = scores_of(0), None
+    for start in range(0, seq_len, Q_BLOCK):
+        following = scores_of(start + Q_BLOCK) if start + Q_BLOCK < seq_len else None
+        weights = weights_of(*scores)
+        if waiting is not None:
+            finish(*waiting)
+        waiting, scores = (start, *weights), following
+    finish(*waiting)
 
 
 def attend(exponent, queries, keys, values, first, heads):
@@ -151,11 +166,17 @@
     )(exponent, queries, keys, values)
 
 
-def product_kernel(*refs, jobs, units, acts):
+def product_kernel(*refs, jobs, units, acts, extra, whole):
     piece_refs = [refs[4 * u : 4 * u + 4] for u in range(units)]
     act_refs = [refs[4 * units + 2 * a : 4 * units + 2 * a + 2] for a in range(acts // 2)]
-    outs = refs[4 * units + acts : 4 * units + acts + 4]
-    grads, values, results, grad_sem, value_sem, result_sem = refs[4 * units + acts + 4 :]
+    refs = refs[4 * units + acts :]
+    extra_refs, refs = refs[:extra], refs[extra:]
+    if whole:
+        outs = [refs[0].at[pl.ds(part * ROWS, ROWS), :] for part in range(NZ)]
+    else:
+        outs = refs[:NZ]
+    grads, values, results, grad_sem, value_sem, result_sem, *added = refs[1 if whole else NZ :]
+    extra_copies = [pltpu.make_async_copy(ref, added[0], added[1].at[0]) for ref in extra_refs]
     yl = position()[3]
     grad_copies = []
     for u in range(units):
@@ -178,16 +199,21 @@
         for seq in range(2)
     ]
     per_unit = len(grad_copies) // units
-    for copy in grad_copies[:per_unit] + value_copies + grad_copies[per_unit:]:
+    ahead = min(AHEAD, acts)
+    for copy in grad_copies[:per_unit] + value_copies[: 2 * ahead] + grad_copies[per_unit:] + extra_copies:
         copy.start()
     waited = 0
     done = 0
     for u in range(units):
         for copy in grad_copies[u * per_unit : (u + 1) * per_unit]:
             copy.wait()
-        for first, count, out_first in jobs[u]:
-
-            def step(j, carry, u=u, first=first, out_first=out_first, waited=waited):
+        for first, count, out_first, extra_first in jobs[u]:
+            if extra_first is not None:
+                for copy in extra_copies:
+                    copy.wait()
+                extra_copies = []
+
+            def step(j, carry, u=u, first=first, out_first=out_first, waited=waited, extra_first=extra_first):
                 @pl.when(first + j >= waited)
                 def _():
                     for seq in range(2):
@@ -196,10 +222,19 @@
                             values.at[first + j, seq],
                             value_sem.at[first + j, seq],
                         ).wait()
+                    for a in range(max(ahead, first + ahead), min(acts, first + count + ahead)):
+
+                        @pl.when(first + j + ahead == a)
+                        def _(a=a):
+                            value_copies[2 * a].start()
+                            value_copies[2 * a + 1].start()
 
                 act = values[first + j].reshape(-1, QUARTER)
                 tile = jnp.dot(grads[u], act, preferred_element_type=jnp.float32)
                 at = out_first + j
+                if extra_first is not None:
+                    start = pl.multiple_of((extra_first + j) * QUARTER, QUARTER)
+                    tile = tile + added[0][:, pl.ds(start, QUARTER)].astype(jnp.float32)
                 results[at] = tile.astype(results.dtype)
                 for part in range(NZ):
                     pltpu.make_async_copy(
@@ -225,18 +260,19 @@
     lax.fori_loop(0, done, settle, 0)
 
 
-def products(pieces, acts, jobs):
+def products(pieces, acts, jobs, extra=(), whole=False):
     units, count = len(pieces), 2 * len(acts)
-    total = sum(n for runs in jobs for _, n, _ in runs)
-    operands = [a for piece in pieces for a in piece] + [a for pair in acts for a in pair]
+    total = sum(n for runs in jobs for _, n, *_ in runs)
+    operands = [a for piece in pieces for a in piece] + [a for pair in acts for a in pair] + list(extra)
     tokens = pieces[0][0].shape[-1]
     shape = acts[0][0].shape[:2] + (QUARTER,)
+    shapes = (NZ * ROWS,) if whole else (ROWS,) * NZ
     flops = 2 * total * QUARTER * NZ * ROWS * 2 * shape[0] * shape[1]
     return pl.pallas_call(
-        functools.partial(product_kernel, jobs=jobs, units=units, acts=count),
+        functools.partial(product_kernel, jobs=jobs, units=units, acts=count, extra=len(extra), whole=whole),
         in_specs=[pl.BlockSpec(memory_space=pl.ANY)] * len(operands),
-        out_specs=[pl.BlockSpec(memory_space=pl.ANY)] * NZ,
-        out_shape=[jax.ShapeDtypeStruct((ROWS, total * QUARTER), jnp.bfloat16)] * NZ,
+        out_specs=[pl.BlockSpec(memory_space=pl.ANY)] * len(shapes),
+        out_shape=[jax.ShapeDtypeStruct((rows, total * QUARTER), jnp.bfloat16) for rows in shapes],
         scratch_shapes=[
             pltpu.VMEM((units, NZ * ROWS, 4 * NX * tokens), jnp.bfloat16),
             pltpu.VMEM((count, 2) + shape, jnp.bfloat16),
@@ -244,7 +280,8 @@
             pltpu.SemaphoreType.DMA((units, 4 * NX)),
             pltpu.SemaphoreType.DMA((count, 2)),
             pltpu.SemaphoreType.DMA((total, NZ)),
-        ],
+        ]
+        + ([pltpu.VMEM((NZ * ROWS, extra[0].shape[1]), jnp.bfloat16), pltpu.SemaphoreType.DMA((1,))] if extra else []),
         cost_estimate=pl.CostEstimate(flops=flops, bytes_accessed=2**20, transcendentals=0),
     )(*operands)
 
@@ -252,28 +289,27 @@
 def reduce_over_z(parts, upward, hold):
     f32 = jnp.float32
     far, up, down, own = parts
-    passing = send(far, Z_UP if upward else Z_DOWN)
+    late, soon = (up, down) if upward else (down, up)
+    onward, back = (Z_UP, Z_DOWN) if upward else (Z_DOWN, Z_UP)
+    passing = send(far, onward)
     if hold is not None:
         passing, _ = lax.optimization_barrier((passing, hold))
-    if upward:
-        below_sent = send((up.astype(f32) + passing.astype(f32)).astype(up.dtype), Z_UP)
-        above_sent = send(down, Z_DOWN)
-    else:
-        above_sent = send((down.astype(f32) + passing.astype(f32)).astype(down.dtype), Z_DOWN)
-        below_sent = send(up, Z_UP)
-    return own, below_sent, above_sent
+    joined = (late.astype(f32) + passing.astype(f32)).astype(late.dtype)
+    soon_sum = send(soon, back)
+    late_sum = send(joined, onward)
+    return own, soon_sum, late_sum, joined
 
 
 HEADS_PER_HALF = 2 * QUARTER // HEAD_DIM
 
 PORTIONS = (
-    ("pa", ((0, "own", 0, 4),)),
-    ("pb", ((0, "y", 0, 2), (1, "own", 0, 4), (1, "y", 0, 2))),
-    ("pc", ((0, "y", 2, 2), (1, "y", 2, 2))),
-    ("pd", ((2, "own", 0, 4), (2, "y", 0, 4))),
-    ("pe", ((3, "own", 0, 4), (3, "y", 0, 4))),
+    ("pa", None, ((0, "own", 0, 4),)),
+    ("pb", True, ((0, "y", 0, 2), (1, "own", 0, 4))),
+    ("pc", False, ((0, "y", 2, 2), (1, "y", 2, 2), (1, "y", 0, 2))),
+    ("pd", False, ((2, "own", 0, 4), (2, "y", 0, 4))),
+    ("pe", True, ((3, "own", 0, 4), (3, "y", 0, 4))),
 )
-OUTER = (("pa", "pb", "pc"), ("pd",))
+OUTER = (("pb", "pc"), ("pd",))
 
 
 def program(saved_queries, saved_keys, saved_values, out_grad, act_exponent, grad_exponent):
@@ -314,7 +350,8 @@
         pieces.append((block, left, right, far))
 
     made = {}
-    for name, runs in PORTIONS:
+    direct = ()
+    for name, upward, runs in PORTIONS:
         units, used, jobs, at = [], [], [], 0
         for unit, side, first, count in runs:
             if unit not in units:
@@ -323,16 +360,23 @@
             for quarter in range(first, first + count):
                 if (side, quarter) not in used:
                     used.append((side, quarter))
-            jobs[units.index(unit)].append((used.index((side, first)), count, at))
+            joins = first if (unit, side) == (1, "y") else None
+            jobs[units.index(unit)].append((used.index((side, first)), count, at, joins))
             at += count
         halves = [acts[side, quarter // 2] for side, quarter in used[::2]]
-        made[name] = products([pieces[u] for u in units], halves, jobs)
+        extra = direct if any(run[3] is not None for runs_of in jobs for run in runs_of) else ()
+        made[name] = products([pieces[u] for u in units], halves, jobs, extra, upward is None)
+        if upward is None:
+            direct = (send(made[name][0], Y_OUTER),)
 
     sums = {}
     leaving = {}
-    for index, (name, runs) in enumerate(PORTIONS):
+    joined = {}
+    for index, (name, upward, runs) in enumerate(PORTIONS):
+        if upward is None:
+            continue
         later = made[PORTIONS[index + 1][0]][3] if index + 1 < len(PORTIONS) else None
-        own, below, above = reduce_over_z(made[name], index % 2 == 0, later)
+        own, below, above, joined[name] = reduce_over_z(made[name], upward, later)
         at = 0
         leaving[name] = []
         for unit, side, first, count in runs:
@@ -349,15 +393,14 @@
             cut = len(leaving[name]) * QUARTER
             own, below, above, _ = sums[leaving[name][0]]
             if index == 0:
-                own, below, above, _ = lax.optimization_barrier((own, below, above, made["pe"][3]))
+                own, below, above, _ = lax.optimization_barrier((own, below, above, joined["pd"]))
             columns.append(own[:, :cut].astype(f32) + below[:, :cut].astype(f32) + above[:, :cut].astype(f32))
             for key in leaving[name]:
                 out_places.append((*key, index, at))
                 at += 1
         message = jnp.concatenate(columns, 1).astype(bf16)
         outgoing[index] = send(message, Y_OUTER)
-        if index:
-            outgoing[0], _ = lax.optimization_barrier((outgoing[0], message))
+        outgoing[index], _ = lax.optimization_barrier((outgoing[index], joined["pe"]))
 
     incoming = {}
     for unit, side, quarter, name, at in out_places:
@@ -367,16 +410,13 @@
         columns = []
         for quarter in range(4):
             own, below, above, at = sums[unit, side, quarter]
-            arrived, there = incoming[unit, side, quarter]
+            parts = [(own, at), (below, at), (above, at)]
+            if (unit, side, quarter) in incoming:
+                parts.append(incoming[unit, side, quarter])
             if hold is not None:
-                own, below, above, arrived, _ = lax.optimization_barrier((own, below, above, arrived, hold))
-            cut = slice(at * QUARTER, (at + 1) * QUARTER)
-            columns.append(
-                own[:, cut].astype(f32)
-                + below[:, cut].astype(f32)
-                + above[:, cut].astype(f32)
-                + arrived[:, there * QUARTER : (there + 1) * QUARTER].astype(f32)
-            )
+                arrays = lax.optimization_barrier((*(a for a, _ in parts), hold))
+                parts = [(a, where) for a, (_, where) in zip(arrays[:-1], parts, strict=True)]
+            columns.append(sum(a[:, w * QUARTER : (w + 1) * QUARTER].astype(f32) for a, w in parts))
         return jnp.concatenate(columns, 1)
 
     keeps, gifts = [], []

time: 248 us -> 238 us (0.960)
  Pallas kernels: 68.6 us -> 58.9 us
  waiting for transfers between devices: 116 us -> 120 us
    pallas_call x2, Pallas kernels: 18 us -> 12.4 us  [attend(): pl.pallas_call(attention_kernel, grid=(heads,), in_specs=[pl.BlockSpec(me...]
    ppermute x50 -> x48, waiting for transfers between devices: 116 us -> 120 us  [send(): return lax.ppermute(block, AXES, pairs)]
    pallas_call x5, Pallas kernels: 44.8 us -> 40.7 us  [products(): pl.pallas_call(functools.partial(product_kernel, jobs=jobs, units=units,...]
    ppermute x50 -> x48, starting transfers between devices: 48.1 us -> 47.4 us  [send(): return lax.ppermute(block, AXES, pairs)]
  transfers between devices with their start and end apart: 50 -> 48, of which waited for: 15 -> 16; matrix products, arithmetic and copies ran while one was open for 3% -> 2% of each run, Pallas kernels for 27% -> 24%
where the time goes in v1:
time: 238 us; the launch traced here: 237 us
  waiting for transfers between devices  120 us (50%)
  Pallas kernels  58.9 us (25%)
  starting transfers between devices  47.4 us (20%)
  other arithmetic  7.15 us (3%)
    ppermute x48, waiting for transfers between devices, send(): return lax.ppermute(block, AXES, pairs)  120 us
    ppermute x48, starting transfers between devices, send(): return lax.ppermute(block, AXES, pairs)  47.4 us
    pallas_call x5, Pallas kernels, products(): pl.pallas_call(functools.partial(product_kernel, jobs=jobs, units=units,...  40.7 us
    pallas_call x2, Pallas kernels, attend(): pl.pallas_call(attention_kernel, grid=(heads,), in_specs=[pl.BlockSpec(me...  12.4 us
    pallas_call x2, Pallas kernels, quantize_columns(): pl.pallas_call(functools.partial(quantize_kernel, made=made), in_specs=[p...  5.82 us
  transfers between devices with their start and end apart: 48, of which 16 were waited for; matrix products, arithmetic and copies ran while one was open for 2% of the time, Pallas kernels for 24%

profile of v1, /device:TPU:0, one launch (start us, length us, event | category | flops | bytes accessed | tf_op | source)
XLA Modules:
  0.0 236.7 jit_solution(8619494143219075357)
XLA Ops:
  0.7 2.5 %shard_map.64 = (bf16[1,512,128]{2,1,0:T(8,128)(2,1)}, bf16[1,512,128]{2,1,0:T(8,128)(2,1)}, bf16[1,512,128]{2,1,0:T(8,128)(2,1)}, bf16[1,512,128]{2,1,0:T(8,128)(2,1)}) custom-call(s32[1]{0:T(128)S(6)} %copy.8.exponent_ref, bf16[128,8192]{1,0:T(8,128)(2,1)} %grad_ref.3), custom_call_target="tpu_custom_call" | custom-call | flops 2000000000 | bytes 3145728 | tf_op jit(solution)/shard_map/pallas_call | solution.py:84
  3.2 3.3 %shard_map.65 = (bf16[3,512,128]{2,1,0:T(8,128)(2,1)}, bf16[1,512,128]{2,1,0:T(8,128)(2,1)}, bf16[2,512,128]{2,1,0:T(8,128)(2,1)}, bf16[1,512,128]{2,1,0:T(8,128...) custom-call(s32[1]{0:T(128)S(6)} %copy.8.exponent_ref, ...), custom_call_target="tpu_custom_call" | custom-call | flops 2000000000 | bytes 3145728 | tf_op jit(solution)/shard_map/pallas_call | solution.py:84
  10.0 6.2 %shard_map.66.refs_10_.refs_4_ = bf16[8,128,512]{2,1,0:T(8,128)(2,1)} custom-call(s32[1]{0:T(128)S(6)} %copy.7.exponent_ref, bf16[1024,1024]{1,0:T(8,128)(2,1)} %query_ref.3, bf16[1024,128]{1,0:T(8,128)(2,1)} %key_ref.3, bf16[1024,128]{1,0:T(8,128)(2,1)} %value_ref.3), custom_call_target="tpu_custom_call" | custom-call | flops 4000000000 | bytes 1048576 | tf_op jit(solution)/shard_map/pallas_call | solution.py:154
  20.6 2.1 collective-permute-done.7
  24.2 28.5 %collective-permute-done.10 = bf16[1,512,128]{2,1,0:T(8,128)(2,1)S(1)} collective-permute-done((bf16[1,512,128]{2,1,0:T(8,128)(2,1)S(1)}, bf16[1,512,128]{2,1,0:T(8,128)(2,1)S(1)}, u32[]{:S(2)}, u32[]{:S(2)}) %collective-permute-start.10) | collective-permute-done | bytes 131104 | tf_op jit(solution)/shard_map/ppermute | solution.py:47
  52.7 2.8 %collective-permute-start.5 = (bf16[2,2,512,128]{3,2,1,0:T(8,128)(2,1)S(1)}, bf16[2,2,512,128]{3,2,1,0:T(8,128)(2,1)}, u32[]{:S(2)}, u32[]{:S(2)}) collective-permute-start(bf16[2,2,512,128]{3,2,1,0:T(8,128)(2,1)S(1)} %bitcast.14), channel_id=1, source_target_pairs={{0,3},{1,0},{2,1},{3,2},{4,7},{5,4},{6,5},{7,6},{8,11},{9,8},{10,9... | collective-permute-start | bytes 1572872 | tf_op jit(solution)/shard_map/ppermute | solution.py:47
  58.1 6.2 %shard_map.67.refs_12_.refs_6_ = bf16[8,128,512]{2,1,0:T(8,128)(2,1)} custom-call(s32[1]{0:T(128)S(6)} %copy.7.exponent_ref, bf16[1024,1024]{1,0:T(8,128)(2,1)} %query_ref.3, bf16[1024,128]{1,0:T(8,128)(2,1)} %key_ref.3, bf16[1024,128]{1,0:T(8,128)(2,1)} %value_ref.3), custom_call_target="tpu_custom_call" | custom-call | flops 4000000000 | bytes 1048576 | tf_op jit(solution)/shard_map/pallas_call | solution.py:154
  64.9 2.9 %collective-permute-done.5.refs_2_ = bf16[2,2,512,128]{3,2,1,0:T(8,128)(2,1)} collective-permute-done((bf16[2,2,512,128]{3,2,1,0:T(8,128)(2,1)S(1)}, bf16[2,2,512,128]{3,2,1,0:T(8,128)(2,1)}, u32[]{:S(2)}, u32[]{:S(2)}) %collective-permute-start.5) | collective-permute-done | bytes 524320 | tf_op jit(solution)/shard_map/ppermute | solution.py:47
  69.4 8.0 %collective-permute-done.12.refs_6_ = bf16[2,2,512,128]{3,2,1,0:T(8,128)(2,1)} collective-permute-done((bf16[2,2,512,128]{3,2,1,0:T(8,128)(2,1)S(1)}, bf16[2,2,512,128]{3,2,1,0:T(8,128)(2,1)}, u32[]{:S(2)}, u32[]{:S(2)}) %collective-permute-start.12) | collective-permute-done | bytes 524320 | tf_op jit(solution)/shard_map/ppermute | solution.py:47
  78.8 12.8 %collective-permute-done.11.refs_5_ = bf16[2,2,512,128]{3,2,1,0:T(8,128)(2,1)S(1)} collective-permute-done((bf16[2,2,512,128]{3,2,1,0:T(8,128)(2,1)S(1)}, bf16[2,2,512,128]{3,2,1,0:T(8,128)(2,1)S(1)}, u32[]{:S(2)}, u32[]{:S(2)}) %collective-permute-start.11) | collective-permute-done | bytes 524320 | tf_op jit(solution)/shard_map/ppermute | solution.py:47
  91.7 3.2 %collective-permute-start.28 = (bf16[2,2,512,128]{3,2,1,0:T(8,128)(2,1)S(1)}, bf16[2,2,512,128]{3,2,1,0:T(8,128)(2,1)S(1)}, u32[]{:S(2)}, u32[]{:S(2)}) collective-permute-start(bf16[2,2,512,128]{3,2,1,0:T(8,128)(2,1)S(1)} %bitcast.23), channel_id=1, source_target_pairs={{0,3},{1,0},{2,1},{3,2},{4,7},{5,4},{6,5},{7,6},{8,11},{9,8},{10,9... | collective-permute-start | bytes 1572872 | tf_op jit(solution)/shard_map/ppermute | solution.py:47
  95.6 12.2 %collective-permute-done.27.refs_1_ = bf16[2,2,512,128]{3,2,1,0:T(8,128)(2,1)} collective-permute-done((bf16[2,2,512,128]{3,2,1,0:T(8,128)(2,1)S(1)}, bf16[2,2,512,128]{3,2,1,0:T(8,128)(2,1)}, u32[]{:S(2)}, u32[]{:S(2)}) %collective-permute-start.27) | collective-permute-done | bytes 524320 | tf_op jit(solution)/shard_map/ppermute | solution.py:47
  109.3 6.5 %collective-permute-done.6.refs_3_ = bf16[2,2,512,128]{3,2,1,0:T(8,128)(2,1)S(1)} collective-permute-done((bf16[2,2,512,128]{3,2,1,0:T(8,128)(2,1)}, bf16[2,2,512,128]{3,2,1,0:T(8,128)(2,1)S(1)}, u32[]{:S(2)}, u32[]{:S(2)}) %collective-permute-start.6) | collective-permute-done | bytes 524320 | tf_op jit(solution)/shard_map/ppermute | solution.py:47
  116.6 6.0 %shard_map.69 = bf16[512,1024]{1,0:T(8,128)(2,1)} custom-call(bf16[2,2,512,128]{3,2,1,0:T(8,128)(2,1)} %bitcast.15, bf16[2,2,512,128]{3,2,1,0:T(8,128)(2,1)} %collective-permute-done.4.refs_1_, bf16[2,2,512,128]{3,2,1,0:T(8,128)(2,1)} %collective-permute-done.5.refs_2_, bf16[2,2,512,128]{3,2,1,0:T(8,128)(2,1)} %copy-done.21, ...), custom_call_target="tpu_custom_call" | custom-call | flops 2147483648 | bytes 1048576 | tf_op jit(solution)/shard_map/pallas_call | solution.py:271
  122.8 7.0 %collective-permute-done.13.refs_7_ = bf16[2,2,512,128]{3,2,1,0:T(8,128)(2,1)} collective-permute-done((bf16[2,2,512,128]{3,2,1,0:T(8,128)(2,1)}, bf16[2,2,512,128]{3,2,1,0:T(8,128)(2,1)}, u32[]{:S(2)}, u32[]{:S(2)}) %collective-permute-start.13) | collective-permute-done | bytes 524320 | tf_op jit(solution)/shard_map/ppermute | solution.py:47
  131.4 2.9 %collective-permute-start.22 = (bf16[512,1024]{1,0:T(8,128)(2,1)}, bf16[512,1024]{1,0:T(8,128)(2,1)}, u32[]{:S(2)}, u32[]{:S(2)}) collective-permute-start(bf16[512,1024]{1,0:T(8,128)(2,1)} %shard_map.69), channel_id=1, source_target_pairs={{0,68},{1,69},{2,70},{3,71},{4,64},{5,65},{6,66},{7,67},{8,76},{9,... | collective-permute-start | bytes 3145736 | tf_op jit(solution)/shard_map/ppermute | solution.py:47
  134.4 8.2 %shard_map.68 = (bf16[128,1536]{1,0:T(8,128)(2,1)}, bf16[128,1536]{1,0:T(8,128)(2,1)}, bf16[128,1536]{1,0:T(8,128)(2,1)}, bf16[128,1536]{1,0:T(8,128)(2,1)}) custom-call(bf16[2,2,512,128]{3,2,1,0:T(8,128)(2,1)} %bitcast.16, bf16[2,2,512,128]{3,2,1,0:T(8,128)(2,1)} %collective-permute-done.4.refs_1_, bf16[2,2,512,128]{3,2,1,0:T(8,128)(2,1)} %collective-permute-done.5.refs_2_, ...), custom_call_target="tpu_custom_call" | custom-call | flops 3221225472 | bytes 1048576 | tf_op jit(solution)/shard_map/pallas_call | solution.py:271
  142.6 2.0 collective-permute-start.19
  144.6 2.2 collective-permute-start.18
  146.8 9.2 %shard_map.71 = (bf16[128,2048]{1,0:T(8,128)(2,1)}, bf16[128,2048]{1,0:T(8,128)(2,1)}, bf16[128,2048]{1,0:T(8,128)(2,1)}, bf16[128,2048]{1,0:T(8,128)(2,1)}) custom-call(bf16[2,2,512,128]{3,2,1,0:T(8,128)(2,1)} %bitcast.24, bf16[2,2,512,128]{3,2,1,0:T(8,128)(2,1)} %collective-permute-done.27.refs_1_, bf16[2,2,512,128]{3,2,1,0:T(8,128)(2,1)} %copy-done.22, ...), custom_call_target="tpu_custom_call" | custom-call | flops 4294967296 | bytes 1048576 | tf_op jit(solution)/shard_map/pallas_call | solution.py:271
  156.0 2.0 collective-permute-start.30
  158.0 9.2 %shard_map.72 = (bf16[128,2048]{1,0:T(8,128)(2,1)}, bf16[128,2048]{1,0:T(8,128)(2,1)}, bf16[128,2048]{1,0:T(8,128)(2,1)}, bf16[128,2048]{1,0:T(8,128)(2,1)}) custom-call(bf16[2,2,512,128]{3,2,1,0:T(8,128)(2,1)} %bitcast.27, bf16[2,2,512,128]{3,2,1,0:T(8,128)(2,1)} %copy-done.23, bf16[2,2,512,128]{3,2,1,0:T(8,128)(2,1)} %collective-permute-done.32.refs_2_, ...), custom_call_target="tpu_custom_call" | custom-call | flops 4294967296 | bytes 1048576 | tf_op jit(solution)/shard_map/pallas_call | solution.py:271
  167.8 8.1 %shard_map.70 = (bf16[128,1536]{1,0:T(8,128)(2,1)}, bf16[128,1536]{1,0:T(8,128)(2,1)}, bf16[128,1536]{1,0:T(8,128)(2,1)}, bf16[128,1536]{1,0:T(8,128)(2,1)}) custom-call(bf16[2,2,512,128]{3,2,1,0:T(8,128)(2,1)} %bitcast.17, bf16[2,2,512,128]{3,2,1,0:T(8,128)(2,1)} %collective-permute-done.4.refs_1_, bf16[2,2,512,128]{3,2,1,0:T(8,128)(2,1)} %collective-permute-done.5.refs_2_, ...), custom_call_target="tpu_custom_call" | custom-call | flops 3221225472 | bytes 1048576 | tf_op jit(solution)/shard_map/pallas_call | solution.py:271
  175.9 3.0 %collective-permute-start.35 = (bf16[128,1536]{1,0:T(8,128)(2,1)}, bf16[128,1536]{1,0:T(8,128)(2,1)S(1)}, u32[]{:S(2)}, u32[]{:S(2)}) collective-permute-start(bf16[128,1536]{1,0:T(8,128)(2,1)} %get-tuple-element.83), channel_id=1, source_target_pairs={{0,48},{1,49},{2,50},{3,51},{4,52},{5,53},{6,54},{7,55},{8,56},{9,... | collective-permute-start | bytes 1179656 | tf_op jit(solution)/shard_map/ppermute | solution.py:47
  179.2 9.5 %collective-permute-done.35 = bf16[128,1536]{1,0:T(8,128)(2,1)S(1)} collective-permute-done((bf16[128,1536]{1,0:T(8,128)(2,1)}, bf16[128,1536]{1,0:T(8,128)(2,1)S(1)}, u32[]{:S(2)}, u32[]{:S(2)}) %collective-permute-start.35) | collective-permute-done | bytes 393248 | tf_op jit(solution)/shard_map/ppermute | solution.py:47
  190.4 2.1 collective-permute-start.36
  192.6 2.1 collective-permute-start.40
  194.7 11.7 %collective-permute-done.23 = bf16[128,1536]{1,0:T(8,128)(2,1)S(1)} collective-permute-done((bf16[128,1536]{1,0:T(8,128)(2,1)S(1)}, bf16[128,1536]{1,0:T(8,128)(2,1)S(1)}, u32[]{:S(2)}, u32[]{:S(2)}) %collective-permute-start.23) | collective-permute-done | bytes 393248 | tf_op jit(solution)/shard_map/ppermute | solution.py:47
  211.4 4.2 %collective-permute-done.43 = bf16[128,2048]{1,0:T(8,128)(2,1)S(1)} collective-permute-done((bf16[128,2048]{1,0:T(8,128)(2,1)S(1)}, bf16[128,2048]{1,0:T(8,128)(2,1)S(1)}, u32[]{:S(2)}, u32[]{:S(2)}) %collective-permute-start.43) | collective-permute-done | bytes 524320 | tf_op jit(solution)/shard_map/ppermute | solution.py:47
  217.8 1.9 collective-permute-done.37
  221.2 3.1 %collective-permute-done.39 = bf16[128,1024]{1,0:T(8,128)(2,1)S(1)} collective-permute-done((bf16[128,1024]{1,0:T(8,128)(2,1)}, bf16[128,1024]{1,0:T(8,128)(2,1)S(1)}, u32[]{:S(2)}, u32[]{:S(2)}) %collective-permute-start.39) | collective-permute-done | bytes 262176 | tf_op jit(solution)/shard_map/ppermute | solution.py:47
  226.8 6.6 %collective-permute-done.45 = bf16[128,1024]{1,0:T(8,128)(2,1)S(1)} collective-permute-done((bf16[128,1024]{1,0:T(8,128)(2,1)S(1)}, bf16[128,1024]{1,0:T(8,128)(2,1)S(1)}, u32[]{:S(2)}, u32[]{:S(2)}) %collective-permute-start.45) | collective-permute-done | bytes 262176 | tf_op jit(solution)/shard_map/ppermute | solution.py:47
  (158 shorter events, 36.6 us)
Async XLA Ops:
  17.9 73.8 %collective-permute-start.14 = (bf16[8,128,512]{2,1,0:T(8,128)(2,1)}, bf16[8,128,512]{2,1,0:T(8,128)(2,1)S(1)}, u32[]{:S(2)}, u32[]{:S(2)}) collective-permute-start(bf16[8,128,512]{2,1,0:T(8,128)(2,1)} %shard_map.66.refs_10_.refs_4_), channel_id=1, source_target_pairs={{0,4},{1,5},{2,6},{3,7},{4,0},{5,1},{6,2},{7,3},{8,12},{9,13},{10,... | collective-permute-start | bytes 3145736 | tf_op jit(solution)/shard_map/ppermute | solution.py:47
  18.3 37.2 %collective-permute-start.25 = (bf16[2,512,128]{2,1,0:T(8,128)(2,1)S(1)}, bf16[2,512,128]{2,1,0:T(8,128)(2,1)}, u32[]{:S(2)}, u32[]{:S(2)}) collective-permute-start(bf16[2,512,128]{2,1,0:T(8,128)(2,1)S(1)} %copy-done.25), channel_id=1, source_target_pairs={{0,8},{1,9},{2,10},{3,11},{4,12},{5,13},{6,14},{7,15},{8,0},{9,1},... | collective-permute-start | bytes 786440 | tf_op jit(solution)/shard_map/ppermute | solution.py:47
  18.4 38.7 %collective-permute-start.24 = (bf16[2,512,128]{2,1,0:T(8,128)(2,1)S(1)}, bf16[2,512,128]{2,1,0:T(8,128)(2,1)S(1)}, u32[]{:S(2)}, u32[]{:S(2)}) collective-permute-start(bf16[2,512,128]{2,1,0:T(8,128)(2,1)S(1)} %copy-done.24), channel_id=1, source_target_pairs={{0,4},{1,5},{2,6},{3,7},{4,0},{5,1},{6,2},{7,3},{8,12},{9,13},{10,... | collective-permute-start | bytes 786440 | tf_op jit(solution)/shard_map/ppermute | solution.py:47
  20.2 32.6 %collective-permute-start.10 = (bf16[1,512,128]{2,1,0:T(8,128)(2,1)S(1)}, bf16[1,512,128]{2,1,0:T(8,128)(2,1)S(1)}, u32[]{:S(2)}, u32[]{:S(2)}) collective-permute-start(bf16[1,512,128]{2,1,0:T(8,128)(2,1)S(1)} %collective-permute-done.9), channel_id=1, source_target_pairs={{0,4},{1,5},{2,6},{3,7},{4,0},{5,1},{6,2},{7,3},{8,12},{9,13},{10,... | collective-permute-start | bytes 393224 | tf_op jit(solution)/shard_map/ppermute | solution.py:47
  22.6 41.8 %collective-permute-start.4 = (bf16[2,2,512,128]{3,2,1,0:T(8,128)(2,1)S(1)}, bf16[2,2,512,128]{3,2,1,0:T(8,128)(2,1)}, u32[]{:S(2)}, u32[]{:S(2)}) collective-permute-start(bf16[2,2,512,128]{3,2,1,0:T(8,128)(2,1)S(1)} %bitcast.13), channel_id=1, source_target_pairs={{0,1},{1,2},{2,3},{3,0},{4,5},{5,6},{6,7},{7,4},{8,9},{9,10},{10,1... | collective-permute-start | bytes 1572872 | tf_op jit(solution)/shard_map/ppermute | solution.py:47
  52.7 15.1 %collective-permute-start.5 = (bf16[2,2,512,128]{3,2,1,0:T(8,128)(2,1)S(1)}, bf16[2,2,512,128]{3,2,1,0:T(8,128)(2,1)}, u32[]{:S(2)}, u32[]{:S(2)}) collective-permute-start(bf16[2,2,512,128]{3,2,1,0:T(8,128)(2,1)S(1)} %bitcast.14), channel_id=1, source_target_pairs={{0,3},{1,0},{2,1},{3,2},{4,7},{5,4},{6,5},{7,6},{8,11},{9,8},{10,9... | collective-permute-start | bytes 1572872 | tf_op jit(solution)/shard_map/ppermute | solution.py:47
  57.2 20.2 %collective-permute-start.12 = (bf16[2,2,512,128]{3,2,1,0:T(8,128)(2,1)S(1)}, bf16[2,2,512,128]{3,2,1,0:T(8,128)(2,1)}, u32[]{:S(2)}, u32[]{:S(2)}) collective-permute-start(bf16[2,2,512,128]{3,2,1,0:T(8,128)(2,1)S(1)} %bitcast.18), channel_id=1, source_target_pairs={{0,3},{1,0},{2,1},{3,2},{4,7},{5,4},{6,5},{7,6},{8,11},{9,8},{10,9... | collective-permute-start | bytes 1572872 | tf_op jit(solution)/shard_map/ppermute | solution.py:47
  64.3 30.6 %collective-permute-start.17 = (bf16[8,128,512]{2,1,0:T(8,128)(2,1)}, bf16[8,128,512]{2,1,0:T(8,128)(2,1)S(1)}, u32[]{:S(2)}, u32[]{:S(2)}) collective-permute-start(bf16[8,128,512]{2,1,0:T(8,128)(2,1)} %shard_map.67.refs_12_.refs_6_), channel_id=1, source_target_pairs={{0,8},{1,9},{2,10},{3,11},{4,12},{5,13},{6,14},{7,15},{8,0},{9,1},... | collective-permute-start | bytes 3145736 | tf_op jit(solution)/shard_map/ppermute | solution.py:47
  64.4 30.5 %collective-permute-start.16 = (bf16[8,128,512]{2,1,0:T(8,128)(2,1)}, bf16[8,128,512]{2,1,0:T(8,128)(2,1)S(1)}, u32[]{:S(2)}, u32[]{:S(2)}) collective-permute-start(bf16[8,128,512]{2,1,0:T(8,128)(2,1)} %shard_map.66.refs_10_.refs_4_), channel_id=1, source_target_pairs={{0,8},{1,9},{2,10},{3,11},{4,12},{5,13},{6,14},{7,15},{8,0},{9,1},... | collective-permute-start | bytes 3145736 | tf_op jit(solution)/shard_map/ppermute | solution.py:47
  67.8 27.2 %collective-permute-start.20 = (bf16[8,128,512]{2,1,0:T(8,128)(2,1)}, bf16[8,128,512]{2,1,0:T(8,128)(2,1)}, u32[]{:S(2)}, u32[]{:S(2)}) collective-permute-start(bf16[8,128,512]{2,1,0:T(8,128)(2,1)} %shard_map.67.refs_12_.refs_6_), channel_id=1, source_target_pairs={{0,4},{1,5},{2,6},{3,7},{4,0},{5,1},{6,2},{7,3},{8,12},{9,13},{10,... | collective-permute-start | bytes 3145736 | tf_op jit(solution)/shard_map/ppermute | solution.py:47
  77.4 14.3 %collective-permute-start.11 = (bf16[2,2,512,128]{3,2,1,0:T(8,128)(2,1)S(1)}, bf16[2,2,512,128]{3,2,1,0:T(8,128)(2,1)S(1)}, u32[]{:S(2)}, u32[]{:S(2)}) collective-permute-start(bf16[2,2,512,128]{3,2,1,0:T(8,128)(2,1)S(1)} %bitcast.19), channel_id=1, source_target_pairs={{0,1},{1,2},{2,3},{3,0},{4,5},{5,6},{6,7},{7,4},{8,9},{9,10},{10,1... | collective-permute-start | bytes 1572872 | tf_op jit(solution)/shard_map/ppermute | solution.py:47
  91.7 16.1 %collective-permute-start.27 = (bf16[2,2,512,128]{3,2,1,0:T(8,128)(2,1)S(1)}, bf16[2,2,512,128]{3,2,1,0:T(8,128)(2,1)}, u32[]{:S(2)}, u32[]{:S(2)}) collective-permute-start(bf16[2,2,512,128]{3,2,1,0:T(8,128)(2,1)S(1)} %bitcast.22), channel_id=1, source_target_pairs={{0,1},{1,2},{2,3},{3,0},{4,5},{5,6},{6,7},{7,4},{8,9},{9,10},{10,1... | collective-permute-start | bytes 1572872 | tf_op jit(solution)/shard_map/ppermute | solution.py:47
  91.7 16.6 %collective-permute-start.28 = (bf16[2,2,512,128]{3,2,1,0:T(8,128)(2,1)S(1)}, bf16[2,2,512,128]{3,2,1,0:T(8,128)(2,1)S(1)}, u32[]{:S(2)}, u32[]{:S(2)}) collective-permute-start(bf16[2,2,512,128]{3,2,1,0:T(8,128)(2,1)S(1)} %bitcast.23), channel_id=1, source_target_pairs={{0,3},{1,0},{2,1},{3,2},{4,7},{5,4},{6,5},{7,6},{8,11},{9,8},{10,9... | collective-permute-start | bytes 1572872 | tf_op jit(solution)/shard_map/ppermute | solution.py:47
  94.9 36.5 %collective-permute-start.15 = (bf16[8,128,512]{2,1,0:T(8,128)(2,1)S(1)}, bf16[8,128,512]{2,1,0:T(8,128)(2,1)S(1)}, u32[]{:S(2)}, u32[]{:S(2)}) collective-permute-start(bf16[8,128,512]{2,1,0:T(8,128)(2,1)S(1)} %collective-permute-done.14.refs_8_.refs_10_), channel_id=1, source_target_pairs={{0,8},{1,9},{2,10},{3,11},{4,12},{5,13},{6,14},{7,15},{8,0},{9,1},... | collective-permute-start | bytes 3145736 | tf_op jit(solution)/shard_map/ppermute | solution.py:47
  94.9 20.8 %collective-permute-start.6 = (bf16[2,2,512,128]{3,2,1,0:T(8,128)(2,1)}, bf16[2,2,512,128]{3,2,1,0:T(8,128)(2,1)S(1)}, u32[]{:S(2)}, u32[]{:S(2)}) collective-permute-start(bf16[2,2,512,128]{3,2,1,0:T(8,128)(2,1)} %collective-permute-done.4.refs_1_), channel_id=1, source_target_pairs={{0,1},{1,2},{2,3},{3,0},{4,5},{5,6},{6,7},{7,4},{8,9},{9,10},{10,1... | collective-permute-start | bytes 1572872 | tf_op jit(solution)/shard_map/ppermute | solution.py:47
  95.0 49.5 %collective-permute-start.21 = (bf16[8,128,512]{2,1,0:T(8,128)(2,1)}, bf16[8,128,512]{2,1,0:T(8,128)(2,1)}, u32[]{:S(2)}, u32[]{:S(2)}) collective-permute-start(bf16[8,128,512]{2,1,0:T(8,128)(2,1)} %collective-permute-done.20.refs_8_.refs_10_), channel_id=1, source_target_pairs={{0,8},{1,9},{2,10},{3,11},{4,12},{5,13},{6,14},{7,15},{8,0},{9,1},... | collective-permute-start | bytes 3145736 | tf_op jit(solution)/shard_map/ppermute | solution.py:47
  107.8 14.9 %collective-permute-start.32 = (bf16[2,2,512,128]{3,2,1,0:T(8,128)(2,1)S(1)}, bf16[2,2,512,128]{3,2,1,0:T(8,128)(2,1)}, u32[]{:S(2)}, u32[]{:S(2)}) collective-permute-start(bf16[2,2,512,128]{3,2,1,0:T(8,128)(2,1)S(1)} %bitcast.25), channel_id=1, source_target_pairs={{0,3},{1,0},{2,1},{3,2},{4,7},{5,4},{6,5},{7,6},{8,11},{9,8},{10,9... | collective-permute-start | bytes 1572872 | tf_op jit(solution)/shard_map/ppermute | solution.py:47
  108.3 21.4 %collective-permute-start.13 = (bf16[2,2,512,128]{3,2,1,0:T(8,128)(2,1)}, bf16[2,2,512,128]{3,2,1,0:T(8,128)(2,1)}, u32[]{:S(2)}, u32[]{:S(2)}) collective-permute-start(bf16[2,2,512,128]{3,2,1,0:T(8,128)(2,1)} %collective-permute-done.12.refs_6_), channel_id=1, source_target_pairs={{0,3},{1,0},{2,1},{3,2},{4,7},{5,4},{6,5},{7,6},{8,11},{9,8},{10,9... | collective-permute-start | bytes 1572872 | tf_op jit(solution)/shard_map/ppermute | solution.py:47
  116.6 26.0 %collective-permute-start.29 = (bf16[2,2,512,128]{3,2,1,0:T(8,128)(2,1)}, bf16[2,2,512,128]{3,2,1,0:T(8,128)(2,1)}, u32[]{:S(2)}, u32[]{:S(2)}) collective-permute-start(bf16[2,2,512,128]{3,2,1,0:T(8,128)(2,1)} %collective-permute-done.27.refs_1_), channel_id=1, source_target_pairs={{0,1},{1,2},{2,3},{3,0},{4,5},{5,6},{6,7},{7,4},{8,9},{9,10},{10,1... | collective-permute-start | bytes 1572872 | tf_op jit(solution)/shard_map/ppermute | solution.py:47
  122.7 33.3 %collective-permute-start.31 = (bf16[2,2,512,128]{3,2,1,0:T(8,128)(2,1)S(1)}, bf16[2,2,512,128]{3,2,1,0:T(8,128)(2,1)S(1)}, u32[]{:S(2)}, u32[]{:S(2)}) collective-permute-start(bf16[2,2,512,128]{3,2,1,0:T(8,128)(2,1)S(1)} %bitcast.26), channel_id=1, source_target_pairs={{0,1},{1,2},{2,3},{3,0},{4,5},{5,6},{6,7},{7,4},{8,9},{9,10},{10,1... | collective-permute-start | bytes 1572872 | tf_op jit(solution)/shard_map/ppermute | solution.py:47
  129.8 28.2 %collective-permute-start.33 = (bf16[2,2,512,128]{3,2,1,0:T(8,128)(2,1)}, bf16[2,2,512,128]{3,2,1,0:T(8,128)(2,1)}, u32[]{:S(2)}, u32[]{:S(2)}) collective-permute-start(bf16[2,2,512,128]{3,2,1,0:T(8,128)(2,1)} %collective-permute-done.32.refs_2_), channel_id=1, source_target_pairs={{0,3},{1,0},{2,1},{3,2},{4,7},{5,4},{6,5},{7,6},{8,11},{9,8},{10,9... | collective-permute-start | bytes 1572872 | tf_op jit(solution)/shard_map/ppermute | solution.py:47
  131.4 35.9 %collective-permute-start.22 = (bf16[512,1024]{1,0:T(8,128)(2,1)}, bf16[512,1024]{1,0:T(8,128)(2,1)}, u32[]{:S(2)}, u32[]{:S(2)}) collective-permute-start(bf16[512,1024]{1,0:T(8,128)(2,1)} %shard_map.69), channel_id=1, source_target_pairs={{0,68},{1,69},{2,70},{3,71},{4,64},{5,65},{6,66},{7,67},{8,76},{9,... | collective-permute-start | bytes 3145736 | tf_op jit(solution)/shard_map/ppermute | solution.py:47
  142.6 33.3 %collective-permute-start.19 = (bf16[128,1536]{1,0:T(8,128)(2,1)}, bf16[128,1536]{1,0:T(8,128)(2,1)S(1)}, u32[]{:S(2)}, u32[]{:S(2)}) collective-permute-start(bf16[128,1536]{1,0:T(8,128)(2,1)} %get-tuple-element.65), channel_id=1, source_target_pairs={{0,16},{1,17},{2,18},{3,19},{4,20},{5,21},{6,22},{7,23},{8,24},{9,... | collective-permute-start | bytes 1179656 | tf_op jit(solution)/shard_map/ppermute | solution.py:47
  144.6 48.1 %collective-permute-start.18 = (bf16[128,1536]{1,0:T(8,128)(2,1)}, bf16[128,1536]{1,0:T(8,128)(2,1)}, u32[]{:S(2)}, u32[]{:S(2)}) collective-permute-start(bf16[128,1536]{1,0:T(8,128)(2,1)} %get-tuple-element.63), channel_id=1, source_target_pairs={{0,48},{1,49},{2,50},{3,51},{4,52},{5,53},{6,54},{7,55},{8,56},{9,... | collective-permute-start | bytes 1179656 | tf_op jit(solution)/shard_map/ppermute | solution.py:47
  156.0 23.0 %collective-permute-start.30 = (bf16[128,2048]{1,0:T(8,128)(2,1)}, bf16[128,2048]{1,0:T(8,128)(2,1)S(1)}, u32[]{:S(2)}, u32[]{:S(2)}) collective-permute-start(bf16[128,2048]{1,0:T(8,128)(2,1)} %get-tuple-element.74), channel_id=1, source_target_pairs={{0,48},{1,49},{2,50},{3,51},{4,52},{5,53},{6,54},{7,55},{8,56},{9,... | collective-permute-start | bytes 1572872 | tf_op jit(solution)/shard_map/ppermute | solution.py:47
  167.2 23.2 %collective-permute-start.38 = (bf16[128,2048]{1,0:T(8,128)(2,1)}, bf16[128,2048]{1,0:T(8,128)(2,1)S(1)}, u32[]{:S(2)}, u32[]{:S(2)}) collective-permute-start(bf16[128,2048]{1,0:T(8,128)(2,1)} %get-tuple-element.90), channel_id=1, source_target_pairs={{0,16},{1,17},{2,18},{3,19},{4,20},{5,21},{6,22},{7,23},{8,24},{9,... | collective-permute-start | bytes 1572872 | tf_op jit(solution)/shard_map/ppermute | solution.py:47
  167.3 44.1 %collective-permute-start.42 = (bf16[128,2048]{1,0:T(8,128)(2,1)}, bf16[128,2048]{1,0:T(8,128)(2,1)S(1)}, u32[]{:S(2)}, u32[]{:S(2)}) collective-permute-start(bf16[128,2048]{1,0:T(8,128)(2,1)} %get-tuple-element.97), channel_id=1, source_target_pairs={{0,16},{1,17},{2,18},{3,19},{4,20},{5,21},{6,22},{7,23},{8,24},{9,... | collective-permute-start | bytes 1572872 | tf_op jit(solution)/shard_map/ppermute | solution.py:47
  179.0 29.1 %collective-permute-start.34 = (bf16[128,1536]{1,0:T(8,128)(2,1)}, bf16[128,1536]{1,0:T(8,128)(2,1)S(1)}, u32[]{:S(2)}, u32[]{:S(2)}) collective-permute-start(bf16[128,1536]{1,0:T(8,128)(2,1)} %get-tuple-element.81), channel_id=1, source_target_pairs={{0,16},{1,17},{2,18},{3,19},{4,20},{5,21},{6,22},{7,23},{8,24},{9,... | collective-permute-start | bytes 1179656 | tf_op jit(solution)/shard_map/ppermute | solution.py:47
  188.7 17.7 %collective-permute-start.23 = (bf16[128,1536]{1,0:T(8,128)(2,1)S(1)}, bf16[128,1536]{1,0:T(8,128)(2,1)S(1)}, u32[]{:S(2)}, u32[]{:S(2)}) collective-permute-start(bf16[128,1536]{1,0:T(8,128)(2,1)S(1)} %add_convert_fusion.4), channel_id=1, source_target_pairs={{0,16},{1,17},{2,18},{3,19},{4,20},{5,21},{6,22},{7,23},{8,24},{9,... | collective-permute-start | bytes 1179656 | tf_op jit(solution)/shard_map/ppermute | solution.py:47
  190.4 19.1 %collective-permute-start.36 = (bf16[128,1536]{1,0:T(8,128)(2,1)S(1)}, bf16[128,1536]{1,0:T(8,128)(2,1)S(1)}, u32[]{:S(2)}, u32[]{:S(2)}) collective-permute-start(bf16[128,1536]{1,0:T(8,128)(2,1)S(1)} %add_convert_fusion.3), channel_id=1, source_target_pairs={{0,48},{1,49},{2,50},{3,51},{4,52},{5,53},{6,54},{7,55},{8,56},{9,... | collective-permute-start | bytes 1179656 | tf_op jit(solution)/shard_map/ppermute | solution.py:47
  192.6 33.7 %collective-permute-start.40 = (bf16[128,2048]{1,0:T(8,128)(2,1)}, bf16[128,2048]{1,0:T(8,128)(2,1)S(1)}, u32[]{:S(2)}, u32[]{:S(2)}) collective-permute-start(bf16[128,2048]{1,0:T(8,128)(2,1)} %get-tuple-element.96), channel_id=1, source_target_pairs={{0,48},{1,49},{2,50},{3,51},{4,52},{5,53},{6,54},{7,55},{8,56},{9,... | collective-permute-start | bytes 1572872 | tf_op jit(solution)/shard_map/ppermute | solution.py:47
  208.1 18.2 %collective-permute-start.41 = (bf16[128,2048]{1,0:T(8,128)(2,1)S(1)}, bf16[128,2048]{1,0:T(8,128)(2,1)S(1)}, u32[]{:S(2)}, u32[]{:S(2)}) collective-permute-start(bf16[128,2048]{1,0:T(8,128)(2,1)S(1)} %add_convert_fusion.1), channel_id=1, source_target_pairs={{0,16},{1,17},{2,18},{3,19},{4,20},{5,21},{6,22},{7,23},{8,24},{9,... | collective-permute-start | bytes 1572872 | tf_op jit(solution)/shard_map/ppermute | solution.py:47
  (45 other events, 643.8 us)

commit v2 on v1

--- a/solution.py
+++ b/solution.py
@@ -286,7 +286,7 @@
     )(*operands)
 
 
-def reduce_over_z(parts, upward, hold):
+def reduce_over_z(parts, upward, hold, pieces=1):
     f32 = jnp.float32
     far, up, down, own = parts
     late, soon = (up, down) if upward else (down, up)
@@ -294,10 +294,14 @@
     passing = send(far, onward)
     if hold is not None:
         passing, _ = lax.optimization_barrier((passing, hold))
-    joined = (late.astype(f32) + passing.astype(f32)).astype(late.dtype)
     soon_sum = send(soon, back)
-    late_sum = send(joined, onward)
-    return own, soon_sum, late_sum, joined
+    width = late.shape[1] // pieces
+    joined, late_sums = [], []
+    for piece in range(pieces):
+        cut = slice(piece * width, (piece + 1) * width)
+        joined.append((late[:, cut].astype(f32) + passing[:, cut].astype(f32)).astype(late.dtype))
+        late_sums.append(send(joined[-1], onward))
+    return own, soon_sum, late_sums, joined[0]
 
 
 HEADS_PER_HALF = 2 * QUARTER // HEAD_DIM
@@ -369,6 +373,9 @@
         if upward is None:
             direct = (send(made[name][0], Y_OUTER),)
 
+    def following_exists(index):
+        return index + 1 < len(PORTIONS)
+
     sums = {}
     leaving = {}
     joined = {}
@@ -376,12 +383,14 @@
         if upward is None:
             continue
         later = made[PORTIONS[index + 1][0]][3] if index + 1 < len(PORTIONS) else None
-        own, below, above, joined[name] = reduce_over_z(made[name], upward, later)
+        pieces_of = 1 if following_exists(index) else 2
+        own, soon, late, joined[name] = reduce_over_z(made[name], upward, later, pieces_of)
         at = 0
         leaving[name] = []
         for unit, side, first, count in runs:
             for k in range(count):
-                sums[unit, side, first + k] = (own, below, above, at)
+                piece, late_at = (0, at) if len(late) == 1 else divmod(at, 4)
+                sums[unit, side, first + k] = (own, soon, late[piece], at, late_at)
                 if unit % 2 == 0:
                     leaving[name].append((unit, side, first + k))
                 at += 1
@@ -391,16 +400,18 @@
         at, columns = 0, []
         for name in names:
             cut = len(leaving[name]) * QUARTER
-            own, below, above, _ = sums[leaving[name][0]]
+            own, below, above, *_ = sums[leaving[name][0]]
             if index == 0:
                 own, below, above, _ = lax.optimization_barrier((own, below, above, joined["pd"]))
             columns.append(own[:, :cut].astype(f32) + below[:, :cut].astype(f32) + above[:, :cut].astype(f32))
             for key in leaving[name]:
-                out_places.append((*key, index, at))
+                out_places.append((*key, (index, at // 4), at % 4))
                 at += 1
-        message = jnp.concatenate(columns, 1).astype(bf16)
-        outgoing[index] = send(message, Y_OUTER)
-        outgoing[index], _ = lax.optimization_barrier((outgoing[index], joined["pe"]))
+        whole = jnp.concatenate(columns, 1)
+        for piece in range(at // 4):
+            message = whole[:, piece * 4 * QUARTER : (piece + 1) * 4 * QUARTER].astype(bf16)
+            arrived = send(message, Y_OUTER)
+            outgoing[index, piece], _ = lax.optimization_barrier((arrived, joined["pe"]))
 
     incoming = {}
     for unit, side, quarter, name, at in out_places:
@@ -409,8 +420,8 @@
     def total(unit, side, hold=None):
         columns = []
         for quarter in range(4):
-            own, below, above, at = sums[unit, side, quarter]
-            parts = [(own, at), (below, at), (above, at)]
+            own, below, above, at, late_at = sums[unit, side, quarter]
+            parts = [(own, at), (below, at), (above, late_at)]
             if (unit, side, quarter) in incoming:
                 parts.append(incoming[unit, side, quarter])
             if hold is not None:

time: 238 us -> 239 us (level)
  waiting for transfers between devices: 120 us -> 124 us
  other arithmetic: 7.15 us -> 3.58 us
    ppermute x48 -> x50, waiting for transfers between devices: 120 us -> 124 us  [send(): return lax.ppermute(block, AXES, pairs)]
    ppermute x48 -> x50, starting transfers between devices: 47.4 us -> 46.9 us  [send(): return lax.ppermute(block, AXES, pairs)]
  transfers between devices with their start and end apart: 48 -> 50, of which waited for: 16 -> 17; matrix products, arithmetic and copies ran while one was open for 2% -> 1% of each run, Pallas kernels for 24% -> 23%
where the time goes in v2:
time: 239 us; the launch traced here: 237 us
  waiting for transfers between devices  124 us (52%)
  Pallas kernels  59 us (25%)
  starting transfers between devices  46.9 us (20%)
  other arithmetic  3.58 us (1%)
    ppermute x50, waiting for transfers between devices, send(): return lax.ppermute(block, AXES, pairs)  124 us
    ppermute x50, starting transfers between devices, send(): return lax.ppermute(block, AXES, pairs)  46.9 us
    pallas_call x5, Pallas kernels, products(): pl.pallas_call(functools.partial(product_kernel, jobs=jobs, units=units,...  40.7 us
    pallas_call x2, Pallas kernels, attend(): pl.pallas_call(attention_kernel, grid=(heads,), in_specs=[pl.BlockSpec(me...  12.5 us
    pallas_call x2, Pallas kernels, quantize_columns(): pl.pallas_call(functools.partial(quantize_kernel, made=made), in_specs=[p...  5.74 us
  transfers between devices with their start and end apart: 50, of which 17 were waited for; matrix products, arithmetic and copies ran while one was open for 1% of the time, Pallas kernels for 23%

profile of v2, /device:TPU:0, one launch (start us, length us, event | category | flops | bytes accessed | tf_op | source)
XLA Modules:
  0.0 237.5 jit_solution(11820889567297064359)
XLA Ops:
  0.7 3.2 %shard_map.65 = (bf16[3,512,128]{2,1,0:T(8,128)(2,1)}, bf16[1,512,128]{2,1,0:T(8,128)(2,1)}, bf16[2,512,128]{2,1,0:T(8,128)(2,1)}, bf16[1,512,128]{2,1,0:T(8,128...) custom-call(s32[1]{0:T(128)S(6)} %copy.8.exponent_ref, ...), custom_call_target="tpu_custom_call" | custom-call | flops 2000000000 | bytes 3145728 | tf_op jit(solution)/shard_map/pallas_call | solution.py:84
  4.3 2.6 %shard_map.64 = (bf16[1,512,128]{2,1,0:T(8,128)(2,1)}, bf16[1,512,128]{2,1,0:T(8,128)(2,1)}, bf16[1,512,128]{2,1,0:T(8,128)(2,1)}, bf16[1,512,128]{2,1,0:T(8,128)(2,1)}) custom-call(s32[1]{0:T(128)S(6)} %copy.8.exponent_ref, bf16[128,8192]{1,0:T(8,128)(2,1)} %grad_ref.3), custom_call_target="tpu_custom_call" | custom-call | flops 2000000000 | bytes 3145728 | tf_op jit(solution)/shard_map/pallas_call | solution.py:84
  9.8 6.3 %shard_map.67.refs_12_.refs_6_ = bf16[8,128,512]{2,1,0:T(8,128)(2,1)} custom-call(s32[1]{0:T(128)S(6)} %copy.7.exponent_ref, bf16[1024,1024]{1,0:T(8,128)(2,1)} %query_ref.3, bf16[1024,128]{1,0:T(8,128)(2,1)} %key_ref.3, bf16[1024,128]{1,0:T(8,128)(2,1)} %value_ref.3), custom_call_target="tpu_custom_call" | custom-call | flops 4000000000 | bytes 1048576 | tf_op jit(solution)/shard_map/pallas_call | solution.py:154
  18.4 6.2 %shard_map.66.refs_10_.refs_4_ = bf16[8,128,512]{2,1,0:T(8,128)(2,1)} custom-call(s32[1]{0:T(128)S(6)} %copy.7.exponent_ref, bf16[1024,1024]{1,0:T(8,128)(2,1)} %query_ref.3, bf16[1024,128]{1,0:T(8,128)(2,1)} %key_ref.3, bf16[1024,128]{1,0:T(8,128)(2,1)} %value_ref.3), custom_call_target="tpu_custom_call" | custom-call | flops 4000000000 | bytes 1048576 | tf_op jit(solution)/shard_map/pallas_call | solution.py:154
  30.5 6.3 %collective-permute-done.10 = bf16[1,512,128]{2,1,0:T(8,128)(2,1)S(1)} collective-permute-done((bf16[1,512,128]{2,1,0:T(8,128)(2,1)S(1)}, bf16[1,512,128]{2,1,0:T(8,128)(2,1)S(1)}, u32[]{:S(2)}, u32[]{:S(2)}) %collective-permute-start.10) | collective-permute-done | bytes 131104 | tf_op jit(solution)/shard_map/ppermute | solution.py:47
  39.0 3.4 %collective-permute-done.26 = bf16[2,512,128]{2,1,0:T(8,128)(2,1)S(1)} collective-permute-done((bf16[2,512,128]{2,1,0:T(8,128)(2,1)S(1)}, bf16[2,512,128]{2,1,0:T(8,128)(2,1)S(1)}, u32[]{:S(2)}, u32[]{:S(2)}) %collective-permute-start.26) | collective-permute-done | bytes 262176 | tf_op jit(solution)/shard_map/ppermute | solution.py:47
  42.4 2.8 %collective-permute-start.12 = (bf16[2,2,512,128]{3,2,1,0:T(8,128)(2,1)S(1)}, bf16[2,2,512,128]{3,2,1,0:T(8,128)(2,1)}, u32[]{:S(2)}, u32[]{:S(2)}) collective-permute-start(bf16[2,2,512,128]{3,2,1,0:T(8,128)(2,1)S(1)} %bitcast.18), channel_id=1, source_target_pairs={{0,3},{1,0},{2,1},{3,2},{4,7},{5,4},{6,5},{7,6},{8,11},{9,8},{10,9... | collective-permute-start | bytes 1572872 | tf_op jit(solution)/shard_map/ppermute | solution.py:47
  45.5 9.1 %collective-permute-done.12.refs_6_ = bf16[2,2,512,128]{3,2,1,0:T(8,128)(2,1)} collective-permute-done((bf16[2,2,512,128]{3,2,1,0:T(8,128)(2,1)S(1)}, bf16[2,2,512,128]{3,2,1,0:T(8,128)(2,1)}, u32[]{:S(2)}, u32[]{:S(2)}) %collective-permute-start.12) | collective-permute-done | bytes 524320 | tf_op jit(solution)/shard_map/ppermute | solution.py:47
  54.6 3.6 %collective-permute-done.31.refs_1_ = bf16[2,2,512,128]{3,2,1,0:T(8,128)(2,1)S(1)} collective-permute-done((bf16[2,2,512,128]{3,2,1,0:T(8,128)(2,1)S(1)}, bf16[2,2,512,128]{3,2,1,0:T(8,128)(2,1)S(1)}, u32[]{:S(2)}, u32[]{:S(2)}) %collective-permute-start.31) | collective-permute-done | bytes 524320 | tf_op jit(solution)/shard_map/ppermute | solution.py:47
  58.5 6.5 %collective-permute-done.14.refs_8_.refs_10_ = bf16[8,128,512]{2,1,0:T(8,128)(2,1)} collective-permute-done((bf16[8,128,512]{2,1,0:T(8,128)(2,1)}, bf16[8,128,512]{2,1,0:T(8,128)(2,1)}, u32[]{:S(2)}, u32[]{:S(2)}) %collective-permute-start.14) | collective-permute-done | bytes 1048608 | tf_op jit(solution)/shard_map/ppermute | solution.py:47
  65.0 21.4 %collective-permute-done.20.refs_8_.refs_10_ = bf16[8,128,512]{2,1,0:T(8,128)(2,1)} collective-permute-done((bf16[8,128,512]{2,1,0:T(8,128)(2,1)S(1)}, bf16[8,128,512]{2,1,0:T(8,128)(2,1)}, u32[]{:S(2)}, u32[]{:S(2)}) %collective-permute-start.20) | collective-permute-done | bytes 1048608 | tf_op jit(solution)/shard_map/ppermute | solution.py:47
  89.6 1.8 collective-permute-start.33
  91.4 11.3 %collective-permute-done.27.refs_1_ = bf16[2,2,512,128]{3,2,1,0:T(8,128)(2,1)} collective-permute-done((bf16[2,2,512,128]{3,2,1,0:T(8,128)(2,1)S(1)}, bf16[2,2,512,128]{3,2,1,0:T(8,128)(2,1)}, u32[]{:S(2)}, u32[]{:S(2)}) %collective-permute-start.27) | collective-permute-done | bytes 524320 | tf_op jit(solution)/shard_map/ppermute | solution.py:47
  103.0 10.9 %collective-permute-done.6.refs_3_ = bf16[2,2,512,128]{3,2,1,0:T(8,128)(2,1)S(1)} collective-permute-done((bf16[2,2,512,128]{3,2,1,0:T(8,128)(2,1)S(1)}, bf16[2,2,512,128]{3,2,1,0:T(8,128)(2,1)S(1)}, u32[]{:S(2)}, u32[]{:S(2)}) %collective-permute-start.6) | collective-permute-done | bytes 524320 | tf_op jit(solution)/shard_map/ppermute | solution.py:47
  115.4 6.1 %shard_map.69 = bf16[512,1024]{1,0:T(8,128)(2,1)} custom-call(bf16[2,2,512,128]{3,2,1,0:T(8,128)(2,1)} %bitcast.15, bf16[2,2,512,128]{3,2,1,0:T(8,128)(2,1)} %copy-done.20, bf16[2,2,512,128]{3,2,1,0:T(8,128)(2,1)} %collective-permute-done.5.refs_2_, bf16[2,2,512,128]{3,2,1,0:T(8,128)(2,1)} %copy-done.21, bf16[8,128,512]{2,1,0:T(8,128)(2,1)} %shard_map.66.refs_10_.refs_4_, ...), custom_call_target="tpu_custom_call" | custom-call | flops 2147483648 | bytes 1048576 | tf_op jit(solution)/shard_map/pallas_call | solution.py:271
  123.6 2.2 collective-permute-start.22
  125.8 9.2 %shard_map.72 = (bf16[128,2048]{1,0:T(8,128)(2,1)}, bf16[128,2048]{1,0:T(8,128)(2,1)}, bf16[128,2048]{1,0:T(8,128)(2,1)}, bf16[128,2048]{1,0:T(8,128)(2,1)}) custom-call(bf16[2,2,512,128]{3,2,1,0:T(8,128)(2,1)} %bitcast.24, bf16[2,2,512,128]{3,2,1,0:T(8,128)(2,1)} %copy-done.22, bf16[2,2,512,128]{3,2,1,0:T(8,128)(2,1)} %collective-permute-done.32.refs_2_, ...), custom_call_target="tpu_custom_call" | custom-call | flops 4294967296 | bytes 1048576 | tf_op jit(solution)/shard_map/pallas_call | solution.py:271
  135.0 2.0 collective-permute-start.38
  137.0 2.2 collective-permute-start.40
  139.2 8.2 %shard_map.68 = (bf16[128,1536]{1,0:T(8,128)(2,1)}, bf16[128,1536]{1,0:T(8,128)(2,1)}, bf16[128,1536]{1,0:T(8,128)(2,1)}, bf16[128,1536]{1,0:T(8,128)(2,1)}) custom-call(bf16[2,2,512,128]{3,2,1,0:T(8,128)(2,1)} %bitcast.16, bf16[2,2,512,128]{3,2,1,0:T(8,128)(2,1)} %copy-done.20, bf16[2,2,512,128]{3,2,1,0:T(8,128)(2,1)} %collective-permute-done.5.refs_2_, ...), custom_call_target="tpu_custom_call" | custom-call | flops 3221225472 | bytes 1048576 | tf_op jit(solution)/shard_map/pallas_call | solution.py:271
  149.0 9.2 %shard_map.71 = (bf16[128,2048]{1,0:T(8,128)(2,1)}, bf16[128,2048]{1,0:T(8,128)(2,1)}, bf16[128,2048]{1,0:T(8,128)(2,1)}, bf16[128,2048]{1,0:T(8,128)(2,1)}) custom-call(bf16[2,2,512,128]{3,2,1,0:T(8,128)(2,1)} %bitcast.27, bf16[2,2,512,128]{3,2,1,0:T(8,128)(2,1)} %collective-permute-done.27.refs_1_, bf16[2,2,512,128]{3,2,1,0:T(8,128)(2,1)} %copy-done.25, ...), custom_call_target="tpu_custom_call" | custom-call | flops 4294967296 | bytes 1048576 | tf_op jit(solution)/shard_map/pallas_call | solution.py:271
  158.2 2.6 %collective-permute-start.30 = (bf16[128,2048]{1,0:T(8,128)(2,1)}, bf16[128,2048]{1,0:T(8,128)(2,1)S(1)}, u32[]{:S(2)}, u32[]{:S(2)}) collective-permute-start(bf16[128,2048]{1,0:T(8,128)(2,1)} %get-tuple-element.75), channel_id=1, source_target_pairs={{0,48},{1,49},{2,50},{3,51},{4,52},{5,53},{6,54},{7,55},{8,56},{9,... | collective-permute-start | bytes 1572872 | tf_op jit(solution)/shard_map/ppermute | solution.py:47
  161.5 8.1 %shard_map.70 = (bf16[128,1536]{1,0:T(8,128)(2,1)}, bf16[128,1536]{1,0:T(8,128)(2,1)}, bf16[128,1536]{1,0:T(8,128)(2,1)}, bf16[128,1536]{1,0:T(8,128)(2,1)}) custom-call(bf16[2,2,512,128]{3,2,1,0:T(8,128)(2,1)} %bitcast.17, bf16[2,2,512,128]{3,2,1,0:T(8,128)(2,1)} %copy-done.20, bf16[2,2,512,128]{3,2,1,0:T(8,128)(2,1)} %collective-permute-done.5.refs_2_, ...), custom_call_target="tpu_custom_call" | custom-call | flops 3221225472 | bytes 1048576 | tf_op jit(solution)/shard_map/pallas_call | solution.py:271
  170.2 3.2 %collective-permute-done.30 = bf16[128,2048]{1,0:T(8,128)(2,1)S(1)} collective-permute-done((bf16[128,2048]{1,0:T(8,128)(2,1)}, bf16[128,2048]{1,0:T(8,128)(2,1)S(1)}, u32[]{:S(2)}, u32[]{:S(2)}) %collective-permute-start.30) | collective-permute-done | bytes 524320 | tf_op jit(solution)/shard_map/ppermute | solution.py:47
  174.4 12.8 %collective-permute-done.35 = bf16[128,1536]{1,0:T(8,128)(2,1)S(1)} collective-permute-done((bf16[128,1536]{1,0:T(8,128)(2,1)}, bf16[128,1536]{1,0:T(8,128)(2,1)S(1)}, u32[]{:S(2)}, u32[]{:S(2)}) %collective-permute-start.35) | collective-permute-done | bytes 393248 | tf_op jit(solution)/shard_map/ppermute | solution.py:47
  187.5 3.1 %collective-permute-start.36 = (bf16[128,1536]{1,0:T(8,128)(2,1)S(1)}, bf16[128,1536]{1,0:T(8,128)(2,1)S(1)}, u32[]{:S(2)}, u32[]{:S(2)}) collective-permute-start(bf16[128,1536]{1,0:T(8,128)(2,1)S(1)} %add_convert_fusion.2), channel_id=1, source_target_pairs={{0,48},{1,49},{2,50},{3,51},{4,52},{5,53},{6,54},{7,55},{8,56},{9,... | collective-permute-start | bytes 1179656 | tf_op jit(solution)/shard_map/ppermute | solution.py:47
  191.0 9.5 %collective-permute-done.23 = bf16[128,1536]{1,0:T(8,128)(2,1)S(1)} collective-permute-done((bf16[128,1536]{1,0:T(8,128)(2,1)S(1)}, bf16[128,1536]{1,0:T(8,128)(2,1)S(1)}, u32[]{:S(2)}, u32[]{:S(2)}) %collective-permute-start.23) | collective-permute-done | bytes 393248 | tf_op jit(solution)/shard_map/ppermute | solution.py:47
  200.4 1.9 collective-permute-start.43
  202.8 8.8 %collective-permute-done.42 = bf16[128,2048]{1,0:T(8,128)(2,1)S(1)} collective-permute-done((bf16[128,2048]{1,0:T(8,128)(2,1)S(1)}, bf16[128,2048]{1,0:T(8,128)(2,1)S(1)}, u32[]{:S(2)}, u32[]{:S(2)}) %collective-permute-start.42) | collective-permute-done | bytes 524320 | tf_op jit(solution)/shard_map/ppermute | solution.py:47
  213.6 9.5 %collective-permute-done.46 = bf16[128,1024]{1,0:T(8,128)(2,1)S(1)} collective-permute-done((bf16[128,1024]{1,0:T(8,128)(2,1)S(1)}, bf16[128,1024]{1,0:T(8,128)(2,1)S(1)}, u32[]{:S(2)}, u32[]{:S(2)}) %collective-permute-start.46) | collective-permute-done | bytes 262176 | tf_op jit(solution)/shard_map/ppermute | solution.py:47
  223.9 2.4 %collective-permute-start.44 = (bf16[128,1024]{1,0:T(8,128)(2,1)S(1)}, bf16[128,1024]{1,0:T(8,128)(2,1)S(1)}, u32[]{:S(2)}, u32[]{:S(2)}) collective-permute-start(bf16[128,1024]{1,0:T(8,128)(2,1)S(1)} %get-tuple-element.123), channel_id=1, source_target_pairs={{0,68},{1,69},{2,70},{3,71},{4,64},{5,65},{6,66},{7,67},{8,76},{9,... | collective-permute-start | bytes 786440 | tf_op jit(solution)/shard_map/ppermute | solution.py:47
  226.6 6.9 %collective-permute-done.44 = bf16[128,1024]{1,0:T(8,128)(2,1)S(1)} collective-permute-done((bf16[128,1024]{1,0:T(8,128)(2,1)S(1)}, bf16[128,1024]{1,0:T(8,128)(2,1)S(1)}, u32[]{:S(2)}, u32[]{:S(2)}) %collective-permute-start.44) | collective-permute-done | bytes 262176 | tf_op jit(solution)/shard_map/ppermute | solution.py:47
  (163 shorter events, 32.4 us)
Async XLA Ops:
  3.8 24.5 %collective-permute-start.25 = (bf16[2,512,128]{2,1,0:T(8,128)(2,1)}, bf16[2,512,128]{2,1,0:T(8,128)(2,1)S(1)}, u32[]{:S(2)}, u32[]{:S(2)}) collective-permute-start(bf16[2,512,128]{2,1,0:T(8,128)(2,1)} %get-tuple-element.71), channel_id=1, source_target_pairs={{0,8},{1,9},{2,10},{3,11},{4,12},{5,13},{6,14},{7,15},{8,0},{9,1},... | collective-permute-start | bytes 786440 | tf_op jit(solution)/shard_map/ppermute | solution.py:47
  3.8 26.2 %collective-permute-start.8 = (bf16[3,512,128]{2,1,0:T(8,128)(2,1)}, bf16[3,512,128]{2,1,0:T(8,128)(2,1)S(1)}, u32[]{:S(2)}, u32[]{:S(2)}) collective-permute-start(bf16[3,512,128]{2,1,0:T(8,128)(2,1)} %get-tuple-element.61), channel_id=1, source_target_pairs={{0,8},{1,9},{2,10},{3,11},{4,12},{5,13},{6,14},{7,15},{8,0},{9,1},... | collective-permute-start | bytes 1179656 | tf_op jit(solution)/shard_map/ppermute | solution.py:47
  26.7 18.6 %collective-permute-start.4 = (bf16[2,2,512,128]{3,2,1,0:T(8,128)(2,1)S(1)}, bf16[2,2,512,128]{3,2,1,0:T(8,128)(2,1)S(1)}, u32[]{:S(2)}, u32[]{:S(2)}) collective-permute-start(bf16[2,2,512,128]{3,2,1,0:T(8,128)(2,1)S(1)} %bitcast.13), channel_id=1, source_target_pairs={{0,1},{1,2},{2,3},{3,0},{4,5},{5,6},{6,7},{7,4},{8,9},{9,10},{10,1... | collective-permute-start | bytes 1572872 | tf_op jit(solution)/shard_map/ppermute | solution.py:47
  28.3 17.1 %collective-permute-start.5 = (bf16[2,2,512,128]{3,2,1,0:T(8,128)(2,1)S(1)}, bf16[2,2,512,128]{3,2,1,0:T(8,128)(2,1)}, u32[]{:S(2)}, u32[]{:S(2)}) collective-permute-start(bf16[2,2,512,128]{3,2,1,0:T(8,128)(2,1)S(1)} %bitcast.14), channel_id=1, source_target_pairs={{0,3},{1,0},{2,1},{3,2},{4,7},{5,4},{6,5},{7,6},{8,11},{9,8},{10,9... | collective-permute-start | bytes 1572872 | tf_op jit(solution)/shard_map/ppermute | solution.py:47
  36.8 28.2 %collective-permute-start.14 = (bf16[8,128,512]{2,1,0:T(8,128)(2,1)}, bf16[8,128,512]{2,1,0:T(8,128)(2,1)}, u32[]{:S(2)}, u32[]{:S(2)}) collective-permute-start(bf16[8,128,512]{2,1,0:T(8,128)(2,1)} %shard_map.66.refs_10_.refs_4_), channel_id=1, source_target_pairs={{0,4},{1,5},{2,6},{3,7},{4,0},{5,1},{6,2},{7,3},{8,12},{9,13},{10,... | collective-permute-start | bytes 3145736 | tf_op jit(solution)/shard_map/ppermute | solution.py:47
  37.2 49.2 %collective-permute-start.20 = (bf16[8,128,512]{2,1,0:T(8,128)(2,1)S(1)}, bf16[8,128,512]{2,1,0:T(8,128)(2,1)}, u32[]{:S(2)}, u32[]{:S(2)}) collective-permute-start(bf16[8,128,512]{2,1,0:T(8,128)(2,1)S(1)} %copy-done.16), channel_id=1, source_target_pairs={{0,4},{1,5},{2,6},{3,7},{4,0},{5,1},{6,2},{7,3},{8,12},{9,13},{10,... | collective-permute-start | bytes 3145736 | tf_op jit(solution)/shard_map/ppermute | solution.py:47
  45.4 42.6 %collective-permute-start.16 = (bf16[8,128,512]{2,1,0:T(8,128)(2,1)S(1)}, bf16[8,128,512]{2,1,0:T(8,128)(2,1)S(1)}, u32[]{:S(2)}, u32[]{:S(2)}) collective-permute-start(bf16[8,128,512]{2,1,0:T(8,128)(2,1)S(1)} %copy-done.17), channel_id=1, source_target_pairs={{0,8},{1,9},{2,10},{3,11},{4,12},{5,13},{6,14},{7,15},{8,0},{9,1},... | collective-permute-start | bytes 3145736 | tf_op jit(solution)/shard_map/ppermute | solution.py:47
  54.6 35.0 %collective-permute-start.17 = (bf16[8,128,512]{2,1,0:T(8,128)(2,1)S(1)}, bf16[8,128,512]{2,1,0:T(8,128)(2,1)S(1)}, u32[]{:S(2)}, u32[]{:S(2)}) collective-permute-start(bf16[8,128,512]{2,1,0:T(8,128)(2,1)S(1)} %copy-done.16), channel_id=1, source_target_pairs={{0,8},{1,9},{2,10},{3,11},{4,12},{5,13},{6,14},{7,15},{8,0},{9,1},... | collective-permute-start | bytes 3145736 | tf_op jit(solution)/shard_map/ppermute | solution.py:47
  58.3 28.2 %collective-permute-start.32 = (bf16[2,2,512,128]{3,2,1,0:T(8,128)(2,1)S(1)}, bf16[2,2,512,128]{3,2,1,0:T(8,128)(2,1)}, u32[]{:S(2)}, u32[]{:S(2)}) collective-permute-start(bf16[2,2,512,128]{3,2,1,0:T(8,128)(2,1)S(1)} %bitcast.23), channel_id=1, source_target_pairs={{0,3},{1,0},{2,1},{3,2},{4,7},{5,4},{6,5},{7,6},{8,11},{9,8},{10,9... | collective-permute-start | bytes 1572872 | tf_op jit(solution)/shard_map/ppermute | solution.py:47
  65.0 57.4 %collective-permute-start.15 = (bf16[8,128,512]{2,1,0:T(8,128)(2,1)}, bf16[8,128,512]{2,1,0:T(8,128)(2,1)}, u32[]{:S(2)}, u32[]{:S(2)}) collective-permute-start(bf16[8,128,512]{2,1,0:T(8,128)(2,1)} %collective-permute-done.14.refs_8_.refs_10_), channel_id=1, source_target_pairs={{0,8},{1,9},{2,10},{3,11},{4,12},{5,13},{6,14},{7,15},{8,0},{9,1},... | collective-permute-start | bytes 3145736 | tf_op jit(solution)/shard_map/ppermute | solution.py:47
  86.4 37.2 %collective-permute-start.21 = (bf16[8,128,512]{2,1,0:T(8,128)(2,1)}, bf16[8,128,512]{2,1,0:T(8,128)(2,1)}, u32[]{:S(2)}, u32[]{:S(2)}) collective-permute-start(bf16[8,128,512]{2,1,0:T(8,128)(2,1)} %collective-permute-done.20.refs_8_.refs_10_), channel_id=1, source_target_pairs={{0,8},{1,9},{2,10},{3,11},{4,12},{5,13},{6,14},{7,15},{8,0},{9,1},... | collective-permute-start | bytes 3145736 | tf_op jit(solution)/shard_map/ppermute | solution.py:47
  86.5 16.2 %collective-permute-start.27 = (bf16[2,2,512,128]{3,2,1,0:T(8,128)(2,1)S(1)}, bf16[2,2,512,128]{3,2,1,0:T(8,128)(2,1)}, u32[]{:S(2)}, u32[]{:S(2)}) collective-permute-start(bf16[2,2,512,128]{3,2,1,0:T(8,128)(2,1)S(1)} %bitcast.25), channel_id=1, source_target_pairs={{0,1},{1,2},{2,3},{3,0},{4,5},{5,6},{6,7},{7,4},{8,9},{9,10},{10,1... | collective-permute-start | bytes 1572872 | tf_op jit(solution)/shard_map/ppermute | solution.py:47
  88.1 25.7 %collective-permute-start.6 = (bf16[2,2,512,128]{3,2,1,0:T(8,128)(2,1)S(1)}, bf16[2,2,512,128]{3,2,1,0:T(8,128)(2,1)S(1)}, u32[]{:S(2)}, u32[]{:S(2)}) collective-permute-start(bf16[2,2,512,128]{3,2,1,0:T(8,128)(2,1)S(1)} %collective-permute-done.4.refs_1_), channel_id=1, source_target_pairs={{0,1},{1,2},{2,3},{3,0},{4,5},{5,6},{6,7},{7,4},{8,9},{9,10},{10,1... | collective-permute-start | bytes 1572872 | tf_op jit(solution)/shard_map/ppermute | solution.py:47
  89.6 31.9 %collective-permute-start.33 = (bf16[2,2,512,128]{3,2,1,0:T(8,128)(2,1)}, bf16[2,2,512,128]{3,2,1,0:T(8,128)(2,1)S(1)}, u32[]{:S(2)}, u32[]{:S(2)}) collective-permute-start(bf16[2,2,512,128]{3,2,1,0:T(8,128)(2,1)} %collective-permute-done.32.refs_2_), channel_id=1, source_target_pairs={{0,3},{1,0},{2,1},{3,2},{4,7},{5,4},{6,5},{7,6},{8,11},{9,8},{10,9... | collective-permute-start | bytes 1572872 | tf_op jit(solution)/shard_map/ppermute | solution.py:47
  102.7 32.3 %collective-permute-start.11 = (bf16[2,2,512,128]{3,2,1,0:T(8,128)(2,1)S(1)}, bf16[2,2,512,128]{3,2,1,0:T(8,128)(2,1)}, u32[]{:S(2)}, u32[]{:S(2)}) collective-permute-start(bf16[2,2,512,128]{3,2,1,0:T(8,128)(2,1)S(1)} %bitcast.19), channel_id=1, source_target_pairs={{0,1},{1,2},{2,3},{3,0},{4,5},{5,6},{6,7},{7,4},{8,9},{9,10},{10,1... | collective-permute-start | bytes 1572872 | tf_op jit(solution)/shard_map/ppermute | solution.py:47
  113.8 23.1 %collective-permute-start.13 = (bf16[2,2,512,128]{3,2,1,0:T(8,128)(2,1)}, bf16[2,2,512,128]{3,2,1,0:T(8,128)(2,1)}, u32[]{:S(2)}, u32[]{:S(2)}) collective-permute-start(bf16[2,2,512,128]{3,2,1,0:T(8,128)(2,1)} %collective-permute-done.12.refs_6_), channel_id=1, source_target_pairs={{0,3},{1,0},{2,1},{3,2},{4,7},{5,4},{6,5},{7,6},{8,11},{9,8},{10,9... | collective-permute-start | bytes 1572872 | tf_op jit(solution)/shard_map/ppermute | solution.py:47
  121.5 25.9 %collective-permute-start.28 = (bf16[2,2,512,128]{3,2,1,0:T(8,128)(2,1)S(1)}, bf16[2,2,512,128]{3,2,1,0:T(8,128)(2,1)S(1)}, u32[]{:S(2)}, u32[]{:S(2)}) collective-permute-start(bf16[2,2,512,128]{3,2,1,0:T(8,128)(2,1)S(1)} %bitcast.26), channel_id=1, source_target_pairs={{0,3},{1,0},{2,1},{3,2},{4,7},{5,4},{6,5},{7,6},{8,11},{9,8},{10,9... | collective-permute-start | bytes 1572872 | tf_op jit(solution)/shard_map/ppermute | solution.py:47
  122.4 25.1 %collective-permute-start.29 = (bf16[2,2,512,128]{3,2,1,0:T(8,128)(2,1)}, bf16[2,2,512,128]{3,2,1,0:T(8,128)(2,1)S(1)}, u32[]{:S(2)}, u32[]{:S(2)}) collective-permute-start(bf16[2,2,512,128]{3,2,1,0:T(8,128)(2,1)} %collective-permute-done.27.refs_1_), channel_id=1, source_target_pairs={{0,1},{1,2},{2,3},{3,0},{4,5},{5,6},{6,7},{7,4},{8,9},{9,10},{10,1... | collective-permute-start | bytes 1572872 | tf_op jit(solution)/shard_map/ppermute | solution.py:47
  123.6 37.2 %collective-permute-start.22 = (bf16[512,1024]{1,0:T(8,128)(2,1)}, bf16[512,1024]{1,0:T(8,128)(2,1)}, u32[]{:S(2)}, u32[]{:S(2)}) collective-permute-start(bf16[512,1024]{1,0:T(8,128)(2,1)} %shard_map.69), channel_id=1, source_target_pairs={{0,68},{1,69},{2,70},{3,71},{4,64},{5,65},{6,66},{7,67},{8,76},{9,... | collective-permute-start | bytes 3145736 | tf_op jit(solution)/shard_map/ppermute | solution.py:47
  135.0 52.5 %collective-permute-start.38 = (bf16[128,2048]{1,0:T(8,128)(2,1)}, bf16[128,2048]{1,0:T(8,128)(2,1)S(1)}, u32[]{:S(2)}, u32[]{:S(2)}) collective-permute-start(bf16[128,2048]{1,0:T(8,128)(2,1)} %get-tuple-element.91), channel_id=1, source_target_pairs={{0,16},{1,17},{2,18},{3,19},{4,20},{5,21},{6,22},{7,23},{8,24},{9,... | collective-permute-start | bytes 1572872 | tf_op jit(solution)/shard_map/ppermute | solution.py:47
  137.0 87.0 %collective-permute-start.40 = (bf16[128,2048]{1,0:T(8,128)(2,1)}, bf16[128,2048]{1,0:T(8,128)(2,1)S(1)}, u32[]{:S(2)}, u32[]{:S(2)}) collective-permute-start(bf16[128,2048]{1,0:T(8,128)(2,1)} %get-tuple-element.97), channel_id=1, source_target_pairs={{0,48},{1,49},{2,50},{3,51},{4,52},{5,53},{6,54},{7,55},{8,56},{9,... | collective-permute-start | bytes 1572872 | tf_op jit(solution)/shard_map/ppermute | solution.py:47
  147.4 22.2 %collective-permute-start.19 = (bf16[128,1536]{1,0:T(8,128)(2,1)}, bf16[128,1536]{1,0:T(8,128)(2,1)S(1)}, u32[]{:S(2)}, u32[]{:S(2)}) collective-permute-start(bf16[128,1536]{1,0:T(8,128)(2,1)} %get-tuple-element.66), channel_id=1, source_target_pairs={{0,16},{1,17},{2,18},{3,19},{4,20},{5,21},{6,22},{7,23},{8,24},{9,... | collective-permute-start | bytes 1179656 | tf_op jit(solution)/shard_map/ppermute | solution.py:47
  158.2 15.2 %collective-permute-start.30 = (bf16[128,2048]{1,0:T(8,128)(2,1)}, bf16[128,2048]{1,0:T(8,128)(2,1)S(1)}, u32[]{:S(2)}, u32[]{:S(2)}) collective-permute-start(bf16[128,2048]{1,0:T(8,128)(2,1)} %get-tuple-element.75), channel_id=1, source_target_pairs={{0,48},{1,49},{2,50},{3,51},{4,52},{5,53},{6,54},{7,55},{8,56},{9,... | collective-permute-start | bytes 1572872 | tf_op jit(solution)/shard_map/ppermute | solution.py:47
  160.8 30.1 %collective-permute-start.18 = (bf16[128,1536]{1,0:T(8,128)(2,1)}, bf16[128,1536]{1,0:T(8,128)(2,1)S(1)}, u32[]{:S(2)}, u32[]{:S(2)}) collective-permute-start(bf16[128,1536]{1,0:T(8,128)(2,1)} %get-tuple-element.64), channel_id=1, source_target_pairs={{0,48},{1,49},{2,50},{3,51},{4,52},{5,53},{6,54},{7,55},{8,56},{9,... | collective-permute-start | bytes 1179656 | tf_op jit(solution)/shard_map/ppermute | solution.py:47
  169.7 17.6 %collective-permute-start.35 = (bf16[128,1536]{1,0:T(8,128)(2,1)}, bf16[128,1536]{1,0:T(8,128)(2,1)S(1)}, u32[]{:S(2)}, u32[]{:S(2)}) collective-permute-start(bf16[128,1536]{1,0:T(8,128)(2,1)} %get-tuple-element.84), channel_id=1, source_target_pairs={{0,48},{1,49},{2,50},{3,51},{4,52},{5,53},{6,54},{7,55},{8,56},{9,... | collective-permute-start | bytes 1179656 | tf_op jit(solution)/shard_map/ppermute | solution.py:47
  173.4 29.0 %collective-permute-start.34 = (bf16[128,1536]{1,0:T(8,128)(2,1)}, bf16[128,1536]{1,0:T(8,128)(2,1)S(1)}, u32[]{:S(2)}, u32[]{:S(2)}) collective-permute-start(bf16[128,1536]{1,0:T(8,128)(2,1)} %get-tuple-element.82), channel_id=1, source_target_pairs={{0,16},{1,17},{2,18},{3,19},{4,20},{5,21},{6,22},{7,23},{8,24},{9,... | collective-permute-start | bytes 1179656 | tf_op jit(solution)/shard_map/ppermute | solution.py:47
  187.2 13.2 %collective-permute-start.23 = (bf16[128,1536]{1,0:T(8,128)(2,1)S(1)}, bf16[128,1536]{1,0:T(8,128)(2,1)S(1)}, u32[]{:S(2)}, u32[]{:S(2)}) collective-permute-start(bf16[128,1536]{1,0:T(8,128)(2,1)S(1)} %add_convert_fusion.3), channel_id=1, source_target_pairs={{0,16},{1,17},{2,18},{3,19},{4,20},{5,21},{6,22},{7,23},{8,24},{9,... | collective-permute-start | bytes 1179656 | tf_op jit(solution)/shard_map/ppermute | solution.py:47
  187.5 15.1 %collective-permute-start.36 = (bf16[128,1536]{1,0:T(8,128)(2,1)S(1)}, bf16[128,1536]{1,0:T(8,128)(2,1)S(1)}, u32[]{:S(2)}, u32[]{:S(2)}) collective-permute-start(bf16[128,1536]{1,0:T(8,128)(2,1)S(1)} %add_convert_fusion.2), channel_id=1, source_target_pairs={{0,48},{1,49},{2,50},{3,51},{4,52},{5,53},{6,54},{7,55},{8,56},{9,... | collective-permute-start | bytes 1179656 | tf_op jit(solution)/shard_map/ppermute | solution.py:47
  190.9 20.8 %collective-permute-start.42 = (bf16[128,2048]{1,0:T(8,128)(2,1)S(1)}, bf16[128,2048]{1,0:T(8,128)(2,1)S(1)}, u32[]{:S(2)}, u32[]{:S(2)}) collective-permute-start(bf16[128,2048]{1,0:T(8,128)(2,1)S(1)} %copy-done.24), channel_id=1, source_target_pairs={{0,16},{1,17},{2,18},{3,19},{4,20},{5,21},{6,22},{7,23},{8,24},{9,... | collective-permute-start | bytes 1572872 | tf_op jit(solution)/shard_map/ppermute | solution.py:47
  202.4 23.9 %collective-permute-start.45 = (bf16[128,1024]{1,0:T(8,128)(2,1)S(1)}, bf16[128,1024]{1,0:T(8,128)(2,1)S(1)}, u32[]{:S(2)}, u32[]{:S(2)}) collective-permute-start(bf16[128,1024]{1,0:T(8,128)(2,1)S(1)} %get-tuple-element.122), channel_id=1, source_target_pairs={{0,16},{1,17},{2,18},{3,19},{4,20},{5,21},{6,22},{7,23},{8,24},{9,... | collective-permute-start | bytes 786440 | tf_op jit(solution)/shard_map/ppermute | solution.py:47
  202.6 30.9 %collective-permute-start.41 = (bf16[128,1024]{1,0:T(8,128)(2,1)S(1)}, bf16[128,1024]{1,0:T(8,128)(2,1)S(1)}, u32[]{:S(2)}, u32[]{:S(2)}) collective-permute-start(bf16[128,1024]{1,0:T(8,128)(2,1)S(1)} %get-tuple-element.121), channel_id=1, source_target_pairs={{0,16},{1,17},{2,18},{3,19},{4,20},{5,21},{6,22},{7,23},{8,24},{9,... | collective-permute-start | bytes 786440 | tf_op jit(solution)/shard_map/ppermute | solution.py:47
  211.7 22.0 %collective-permute-start.39 = (bf16[128,1024]{1,0:T(8,128)(2,1)S(1)}, bf16[128,1024]{1,0:T(8,128)(2,1)S(1)}, u32[]{:S(2)}, u32[]{:S(2)}) collective-permute-start(bf16[128,1024]{1,0:T(8,128)(2,1)S(1)} %pad_maximum_fusion.7), channel_id=1, source_target_pairs={{0,4},{1,5},{2,6},{3,7},{4,0},{5,1},{6,2},{7,3},{8,12},{9,13},{10,... | collective-permute-start | bytes 786440 | tf_op jit(solution)/shard_map/ppermute | solution.py:47
  (47 other events, 873.4 us)
